TPU v7x, 16 devices: a 4x2x1 block of a 4x4x8 slice. The times are simulated.
16 devices in a mesh: sys: 2 (over y, z), row: 8 (over x, core).
Axes of the slice: x: 4, y: 2, z: 1, core: 2. Of those that a mesh axis runs over, the one named last changes fastest.
The devices are a block of a 4x4x8 slice.
Arguments:
- positions: bfloat16 [32768, 256], P(('sys', 'row')), parts along dimension 0
- charges: float32 [32768], P(('sys', 'row')), parts along dimension 0
Outputs:
- output 1: float32 [32768, 256], P(('sys', 'row')), parts along dimension 0
- output 2: float32 [2], P('sys'), parts along dimension 0
There are 2 independent parts. A program takes and returns all parts, laid end to end along the dimension named above; each array names one.
All inputs are finite; a program needn't handle non-finite values.
Results may differ from a plain program's by a relative error of at most 0.001.
Values are sent between devices in bfloat16 or wider.
A program may use at most 768 MiB of HBM per device.

v0:
```python
import jax
import jax.numpy as jnp
from jax import lax
from jax.sharding import PartitionSpec as P


def pair_weight(host_x, host_q, host_sq, vis_x, vis_q, vis_sq, ell_sq):
    cross_dot = lax.dot_general(host_x, vis_x, (((1,), (1,)), ((), ())), preferred_element_type=jnp.float32)
    sq_dist = jnp.maximum(host_sq[:, None] + vis_sq[None, :] - 2.0 * cross_dot, 0.0)
    return host_q[:, None] * vis_q[None, :] * jnp.exp(-sq_dist / (2.0 * ell_sq))


def pair_forces(weight, host_x, vis_x):
    weight_bf = weight.astype(jnp.bfloat16)
    host_force = jnp.sum(weight, axis=1)[:, None] * host_x - jnp.dot(weight_bf, vis_x, preferred_element_type=jnp.float32)
    vis_force = jnp.sum(weight, axis=0)[:, None] * vis_x - lax.dot_general(weight_bf, host_x, (((0,), (0,)), ((), ())), preferred_element_type=jnp.float32)
    return host_force, vis_force


def row_sq(block_x):
    return jnp.sum(jnp.square(block_x.astype(jnp.float32)), axis=1)


def solution(mesh):
    row_count = mesh.shape["row"]
    full_steps = (row_count - 1) // 2
    has_middle = row_count % 2 == 0
    travel = row_count // 2
    forward = [(source, (source + 1) % row_count) for source in range(row_count)]
    homeward = [(source, (source - travel) % row_count) for source in range(row_count)]

    def device_body(pos_loc, chg_loc):
        rows_dev, feat_width = pos_loc.shape
        ell_sq = float(feat_width)
        half_rows = rows_dev // 2
        sq_loc = row_sq(pos_loc)
        local_ids = jnp.arange(rows_dev)
        diag_w = pair_weight(pos_loc, chg_loc, sq_loc, pos_loc, chg_loc, sq_loc, ell_sq)
        diag_w = jnp.where(local_ids[:, None] == local_ids[None, :], 0.0, diag_w)
        own_force = jnp.sum(diag_w, axis=1)[:, None] * pos_loc - jnp.dot(diag_w.astype(jnp.bfloat16), pos_loc, preferred_element_type=jnp.float32)
        own_energy = 0.5 * jnp.sum(diag_w)

        def full_step(step_idx, loop_state):
            vis_x, vis_q, vis_acc, force_acc, energy_acc = loop_state
            vis_x = lax.ppermute(vis_x, "row", forward)
            vis_q = lax.ppermute(vis_q, "row", forward)
            vis_acc = lax.ppermute(vis_acc, "row", forward)
            weight = pair_weight(pos_loc, chg_loc, sq_loc, vis_x, vis_q, row_sq(vis_x), ell_sq)
            host_force, vis_force = pair_forces(weight, pos_loc, vis_x)
            return (vis_x, vis_q, vis_acc + vis_force, force_acc + host_force, energy_acc + jnp.sum(weight))

        loop_state = (pos_loc, chg_loc, jnp.zeros((rows_dev, feat_width), jnp.float32), own_force, own_energy)
        vis_x, vis_q, vis_acc, force_acc, energy_acc = lax.fori_loop(0, full_steps, full_step, loop_state)
        if has_middle:
            vis_x = lax.ppermute(vis_x, "row", forward)
            vis_q = lax.ppermute(vis_q, "row", forward)
            vis_acc = lax.ppermute(vis_acc, "row", forward)
            vis_sq = row_sq(vis_x)
            low_half = lax.axis_index("row") < travel
            part_x = jnp.where(low_half, pos_loc[:half_rows], vis_x[half_rows:])
            part_q = jnp.where(low_half, chg_loc[:half_rows], vis_q[half_rows:])
            part_sq = jnp.where(low_half, sq_loc[:half_rows], vis_sq[half_rows:])
            other_x = jnp.where(low_half, vis_x, pos_loc)
            other_q = jnp.where(low_half, vis_q, chg_loc)
            other_sq = jnp.where(low_half, vis_sq, sq_loc)
            weight = pair_weight(part_x, part_q, part_sq, other_x, other_q, other_sq, ell_sq)
            part_force, other_force = pair_forces(weight, part_x, other_x)
            zero_half = jnp.zeros((half_rows, feat_width), jnp.float32)
            head_fill = jnp.concatenate([part_force, zero_half], axis=0)
            tail_fill = jnp.concatenate([zero_half, part_force], axis=0)
            force_acc = force_acc + jnp.where(low_half, head_fill, other_force)
            vis_acc = vis_acc + jnp.where(low_half, other_force, tail_fill)
            energy_acc = energy_acc + jnp.sum(weight)
        home_acc = lax.ppermute(vis_acc, "row", homeward)
        energy = lax.psum(energy_acc, "row")
        return (force_acc + home_acc) / ell_sq, energy.reshape(1)

    return jax.shard_map(device_body, mesh=mesh, in_specs=(P(("sys", "row"), None), P(("sys", "row"))), out_specs=(P(("sys", "row"), None), P("sys")), check_vma=False)
```

profile of v0, /device:TPU:113, one launch (start us, length us, event | category | flops | bytes accessed | tf_op | source)
XLA Modules:
  0.0 261.5 jit_solution(8157282159709560793)
XLA Ops:
  0.6 1.6 fusion.12
  2.2 2.3 copy.5
  4.6 0.7 copy.6
  5.3 14.1 %fusion.20 = (f32[]{:T(128)}, f32[2048]{0:T(1024)S(1)}, bf16[2048,2048]{0,1:T(8,128)(2,1)}) fusion(bf16[2048,256]{1,0:T(8,128)(2,1)} %param.4, f32[2048]{0:T(1024)S(1)} %fusion.12, f32[2048]{0:T(1024)} %param.5), kind=kOutput, calls=%fused_computation.37 | convolution fusion | flops 2202007552 | bytes 9461764 | tf_op jit(solution)/shard_map/dot_general | solution.py:8
  19.4 8.0 %fusion.9 = f32[2048,256]{1,0:T(8,128)} fusion(bf16[2048,256]{1,0:T(8,128)(2,1)} %param.4, bf16[2048,2048]{0,1:T(8,128)(2,1)} %get-tuple-element.115, f32[2048]{0:T(1024)S(1)} %get-tuple-element.92), kind=kOutput, calls=%fused_computation.19 | convolution fusion | flops 2149056512 | bytes 11542528 | tf_op jit(solution)/shard_map/dot_general | solution.py:40
  27.9 131.1 %while.19 = (s32[]{:T(128)}, bf16[2048,256]{1,0:T(8,128)(2,1)}, f32[2048]{0:T(1024)S(1)}, f32[2048,256]{1,0:T(8,128)}, f32[2048,256]{1,0:T(8,128)}, /*index=5*/f...) while((s32[]{:T(128)}, bf16[2048,256]{1,0:T(8,128)(2,1)}, ...), condition=%wide.region_8.9_spmd.clone, body=%wide.region_3.8_spmd.clone.sunk | while | flops 6499067904 | bytes 85057840 | solution.py:53
  28.1 2.7 %collective-permute-start = (bf16[2048,256]{1,0:T(8,128)(2,1)}, bf16[2048,256]{1,0:T(8,128)(2,1)S(1)}, u32[]{:S(2)}, u32[]{:S(2)}) collective-permute-start(bf16[2048,256]{1,0:T(8,128)(2,1)} %get-tuple-element.205), channel_id=1, source_target_pairs={{0,1},{1,2},{2,3},{3,4},{4,5},{5,6},{6,7},{7,0},{8,9},{9,10},{10,1... | collective-permute-start | bytes 3145736 | tf_op jit(solution)/shard_map/while/body/eval_jaxpr/ppermute | solution.py:45
  30.8 0.1 collective-permute-start.1
  30.9 0.1 broadcast_select_fusion.5
  31.0 1.7 collective-permute-start.2
  32.7 9.9 %collective-permute-done.1 = f32[2048]{0:T(1024)S(1)} collective-permute-done((f32[2048]{0:T(1024)S(1)}, f32[2048]{0:T(1024)S(1)}, u32[]{:S(2)}, u32[]{:S(2)}) %collective-permute-start.1) | collective-permute-done | bytes 8224 | tf_op jit(solution)/shard_map/while/body/eval_jaxpr/ppermute | solution.py:46
  42.6 0.3 fusion.53
  43.0 12.1 %fusion.54 = (f32[]{:T(128)}, f32[2048]{0:T(1024)S(1)}, f32[2048]{0:T(1024)S(1)}, bf16[2048,2048]{1,0:T(8,128)(2,1)}) fusion(bf16[2048,256]{1,0:T(8,128)(2,1)} %get-tuple-element.223, bf16[2048,256]{1,0:T(8,128)(2,1)S(1)} %collective-permute-done, f32[2048]{0:T(1024)S(1)} %fusion.53, f32[2048]{0:T(1024)S(1)} %get-tuple-element.222, ...), kind=kOutput, calls=%fused_computation.36.clone.1 | convolution fusion | flops 2197811200 | bytes 10534916 | tf_op jit(solution)/shard_map/while/body/eval_jaxpr/dot_general | solution.py:8
  55.8 1.1 copy.17
  56.9 8.6 %subtract_add_fusion.2 = f32[2048,256]{1,0:T(8,128)} fusion(f32[2048,256]{1,0:T(8,128)} %get-tuple-element.208, bf16[2048,256]{1,0:T(8,128)(2,1)} %get-tuple-element.223, f32[2048]{0:T(1024)S(1)} %get-tuple-element.191, bf16[2048,256]{1,0:T(8,128)(2,1)S(1)} %collective-permute-done, bf16[2048,2048]{1,0:T(8,128)(2,1)} %get-tuple-element.190), kind=kOutput, calls=%fused_computation.10.clone.1 | convolution fusion | flops 2149580800 | bytes 14688256 | tf_op jit(solution)/shard_map/while/body/eval_jaxpr/dot_general | solution.py:15
  65.5 6.4 %fusion.55 = f32[2048,256]{1,0:T(8,128)} fusion(f32[2048,256]{1,0:T(8,128)} %collective-permute-done.2, bf16[2048,256]{1,0:T(8,128)(2,1)S(1)} %collective-permute-done, f32[2048]{0:T(1024)S(1)} %get-tuple-element.189, bf16[2048,256]{1,0:T(8,128)(2,1)} %get-tuple-element.223, bf16[2048,2048]{1,0:T(8,128)(2,1)S(1)} %bitcast.30), kind=kOutput, calls=%fused_computation.9.clone.1 | convolution fusion | flops 2149580800 | bytes 14688256 | tf_op jit(solution)/shard_map/while/body/eval_jaxpr/dot_general | solution.py:16
  71.9 2.5 collective-permute-start
  74.4 1.7 broadcast_select_fusion.5
  76.1 1.8 collective-permute-start.2
  77.9 8.3 %collective-permute-done.1 = f32[2048]{0:T(1024)S(1)} collective-permute-done((f32[2048]{0:T(1024)S(1)}, f32[2048]{0:T(1024)S(1)}, u32[]{:S(2)}, u32[]{:S(2)}) %collective-permute-start.1) | collective-permute-done | bytes 8224 | tf_op jit(solution)/shard_map/while/body/eval_jaxpr/ppermute | solution.py:46
  86.2 0.3 fusion.53
  86.5 12.1 %fusion.54 = (f32[]{:T(128)}, f32[2048]{0:T(1024)S(1)}, f32[2048]{0:T(1024)S(1)}, bf16[2048,2048]{1,0:T(8,128)(2,1)}) fusion(bf16[2048,256]{1,0:T(8,128)(2,1)} %get-tuple-element.223, bf16[2048,256]{1,0:T(8,128)(2,1)S(1)} %collective-permute-done, f32[2048]{0:T(1024)S(1)} %fusion.53, f32[2048]{0:T(1024)S(1)} %get-tuple-element.222, ...), kind=kOutput, calls=%fused_computation.36.clone.1 | convolution fusion | flops 2197811200 | bytes 10534916 | tf_op jit(solution)/shard_map/while/body/eval_jaxpr/dot_general | solution.py:8
  99.4 1.1 copy.17
  100.4 8.6 %subtract_add_fusion.2 = f32[2048,256]{1,0:T(8,128)} fusion(f32[2048,256]{1,0:T(8,128)} %get-tuple-element.208, bf16[2048,256]{1,0:T(8,128)(2,1)} %get-tuple-element.223, f32[2048]{0:T(1024)S(1)} %get-tuple-element.191, bf16[2048,256]{1,0:T(8,128)(2,1)S(1)} %collective-permute-done, bf16[2048,2048]{1,0:T(8,128)(2,1)} %get-tuple-element.190), kind=kOutput, calls=%fused_computation.10.clone.1 | convolution fusion | flops 2149580800 | bytes 14688256 | tf_op jit(solution)/shard_map/while/body/eval_jaxpr/dot_general | solution.py:15
  109.1 6.4 %fusion.55 = f32[2048,256]{1,0:T(8,128)} fusion(f32[2048,256]{1,0:T(8,128)} %collective-permute-done.2, bf16[2048,256]{1,0:T(8,128)(2,1)S(1)} %collective-permute-done, f32[2048]{0:T(1024)S(1)} %get-tuple-element.189, bf16[2048,256]{1,0:T(8,128)(2,1)} %get-tuple-element.223, bf16[2048,2048]{1,0:T(8,128)(2,1)S(1)} %bitcast.30), kind=kOutput, calls=%fused_computation.9.clone.1 | convolution fusion | flops 2149580800 | bytes 14688256 | tf_op jit(solution)/shard_map/while/body/eval_jaxpr/dot_general | solution.py:16
  115.4 2.5 collective-permute-start
  117.9 0.0 collective-permute-start.1
  117.9 1.7 broadcast_select_fusion.5
  119.7 1.8 collective-permute-start.2
  121.4 8.3 %collective-permute-done.1 = f32[2048]{0:T(1024)S(1)} collective-permute-done((f32[2048]{0:T(1024)S(1)}, f32[2048]{0:T(1024)S(1)}, u32[]{:S(2)}, u32[]{:S(2)}) %collective-permute-start.1) | collective-permute-done | bytes 8224 | tf_op jit(solution)/shard_map/while/body/eval_jaxpr/ppermute | solution.py:46
  129.7 0.3 fusion.53
  130.1 12.1 %fusion.54 = (f32[]{:T(128)}, f32[2048]{0:T(1024)S(1)}, f32[2048]{0:T(1024)S(1)}, bf16[2048,2048]{1,0:T(8,128)(2,1)}) fusion(bf16[2048,256]{1,0:T(8,128)(2,1)} %get-tuple-element.223, bf16[2048,256]{1,0:T(8,128)(2,1)S(1)} %collective-permute-done, f32[2048]{0:T(1024)S(1)} %fusion.53, f32[2048]{0:T(1024)S(1)} %get-tuple-element.222, ...), kind=kOutput, calls=%fused_computation.36.clone.1 | convolution fusion | flops 2197811200 | bytes 10534916 | tf_op jit(solution)/shard_map/while/body/eval_jaxpr/dot_general | solution.py:8
  142.9 1.1 copy.17
  144.0 8.6 %subtract_add_fusion.2 = f32[2048,256]{1,0:T(8,128)} fusion(f32[2048,256]{1,0:T(8,128)} %get-tuple-element.208, bf16[2048,256]{1,0:T(8,128)(2,1)} %get-tuple-element.223, f32[2048]{0:T(1024)S(1)} %get-tuple-element.191, bf16[2048,256]{1,0:T(8,128)(2,1)S(1)} %collective-permute-done, bf16[2048,2048]{1,0:T(8,128)(2,1)} %get-tuple-element.190), kind=kOutput, calls=%fused_computation.10.clone.1 | convolution fusion | flops 2149580800 | bytes 14688256 | tf_op jit(solution)/shard_map/while/body/eval_jaxpr/dot_general | solution.py:15
  152.6 6.4 %fusion.55 = f32[2048,256]{1,0:T(8,128)} fusion(f32[2048,256]{1,0:T(8,128)} %collective-permute-done.2, bf16[2048,256]{1,0:T(8,128)(2,1)S(1)} %collective-permute-done, f32[2048]{0:T(1024)S(1)} %get-tuple-element.189, bf16[2048,256]{1,0:T(8,128)(2,1)} %get-tuple-element.223, bf16[2048,2048]{1,0:T(8,128)(2,1)S(1)} %bitcast.30), kind=kOutput, calls=%fused_computation.9.clone.1 | convolution fusion | flops 2149580800 | bytes 14688256 | tf_op jit(solution)/shard_map/while/body/eval_jaxpr/dot_general | solution.py:16
  159.0 2.5 collective-permute-start.4
  161.5 1.7 collective-permute-start.5
  163.2 10.1 %collective-permute-done.3 = f32[2048]{0:T(1024)S(1)} collective-permute-done((f32[2048]{0:T(1024)S(1)}, f32[2048]{0:T(1024)S(1)}, u32[]{:S(2)}, u32[]{:S(2)}) %collective-permute-start.3) | collective-permute-done | bytes 8224 | tf_op jit(solution)/shard_map/ppermute | solution.py:56
  173.3 0.3 multiply_reduce_fusion
  173.7 1.1 slice_select_fusion
  174.8 0.2 broadcast_select_fusion.1
  175.0 5.4 %fusion.21 = (f32[]{:T(128)}, f32[2048]{0:T(1024)S(1)}, f32[1024]{0:T(1024)S(1)}, bf16[1024,2048]{1,0:T(8,128)(2,1)S(1)}) fusion(bf16[1024,256]{1,0:T(8,128)(2,1)S(1)} %slice_select_fusion, bf16[2048,256]{1,0:T(8,128)(2,1)S(1)} %broadcast_select_fusion.1, f32[2048]{0:T(1024)S(1)} %broadcast_select_fusion.2, f32[1024]{0:T(1024)S(1)} %slice_select_fusion.1, ...), kind=kOutput, calls=%fused_computation.38 | convolution fusion | flops 1098904576 | bytes 5804036 | tf_op jit(solution)/shard_map/dot_general | solution.py:8
  180.3 1.3 multiply_subtract_fusion.1
  181.6 14.1 %collective-permute-done.5 = f32[2048,256]{1,0:T(8,128)} collective-permute-done((f32[2048,256]{1,0:T(8,128)}, f32[2048,256]{1,0:T(8,128)}, u32[]{:S(2)}, u32[]{:S(2)}) %collective-permute-start.5) | collective-permute-done | bytes 2097184 | tf_op jit(solution)/shard_map/ppermute | solution.py:57
  195.7 4.7 %select_add_fusion = (f32[2048,256]{1,0:T(8,128)}, f32[2048,256]{1,0:T(8,128)S(1)}) fusion(f32[2048,256]{1,0:T(8,128)} %collective-permute-done.5, f32[1024,256]{1,0:T(8,128)S(1)} %multiply_subtract_fusion.1, pred[]{:T(512)S(6)} %lt.6, bf16[1024,256]{1,0:T(8,128)(2,1)S(1)} %slice_select_fusion, bf16[1024,2048]{1,0:T(8,128)(2,1)S(1)} %get-tuple-element.116, ...), kind=kOutput, calls=%fused_computation.22 | convolution fusion | flops 1076363264 | bytes 13115393 | tf_op jit(solution)/shard_map/dot_general | solution.py:16
  200.4 2.7 %collective-permute-start.6 = (f32[2048,256]{1,0:T(8,128)}, f32[2048,256]{1,0:T(8,128)}, u32[]{:S(2)}, u32[]{:S(2)}) collective-permute-start(f32[2048,256]{1,0:T(8,128)} %get-tuple-element.117), channel_id=1, source_target_pairs={{0,4},{1,5},{2,6},{3,7},{4,0},{5,1},{6,2},{7,3},{8,12},{9,13},{10,... | collective-permute-start | bytes 6291464 | tf_op jit(solution)/shard_map/ppermute | solution.py:74
  203.8 53.4 %psum.7 = f32[1]{0:T(128)} all-reduce(f32[1]{0:T(128)} %bitcast), channel_id=1, replica_groups=mesh['sys'=2,'row'=8] {'row'}, use_global_device_ids=true, to_apply=%region_13.14 | all-reduce | flops 1 | bytes 8 | tf_op jit(solution)/shard_map/psum | solution.py:75
  257.2 4.3 %add_multiply_fusion = f32[2048,256]{1,0:T(8,128)} fusion(f32[2048,256]{1,0:T(8,128)} %collective-permute-done.6, f32[2048,256]{1,0:T(8,128)} %get-tuple-element.53, f32[2048,256]{1,0:T(8,128)S(1)} %get-tuple-element.118, f32[1024,256]{1,0:T(8,128)S(1)} %multiply_subtract_fusion.1, pred[]{:T(512)S(6)} %lt.6), kind=kLoop, calls=%fused_computation.21 | loop fusion | flops 2097152 | bytes 9437185 | tf_op jit(solution)/shard_map/div | solution.py:76
  (35 shorter events, 0.1 us)
Async XLA Ops:
  19.4 8.6 %copy-start = (f32[2048]{0:T(1024)S(1)}, f32[2048]{0:T(1024)}, u32[]{:S(2)}) copy-start(f32[2048]{0:T(1024)} %param.5) | copy-start | bytes 24580
  28.1 14.5 %collective-permute-start = (bf16[2048,256]{1,0:T(8,128)(2,1)}, bf16[2048,256]{1,0:T(8,128)(2,1)S(1)}, u32[]{:S(2)}, u32[]{:S(2)}) collective-permute-start(bf16[2048,256]{1,0:T(8,128)(2,1)} %get-tuple-element.205), channel_id=1, source_target_pairs={{0,1},{1,2},{2,3},{3,4},{4,5},{5,6},{6,7},{7,0},{8,9},{9,10},{10,1... | collective-permute-start | bytes 3145736 | tf_op jit(solution)/shard_map/while/body/eval_jaxpr/ppermute | solution.py:45
  30.8 11.8 %collective-permute-start.1 = (f32[2048]{0:T(1024)S(1)}, f32[2048]{0:T(1024)S(1)}, u32[]{:S(2)}, u32[]{:S(2)}) collective-permute-start(f32[2048]{0:T(1024)S(1)} %get-tuple-element.206), channel_id=1, source_target_pairs={{0,1},{1,2},{2,3},{3,4},{4,5},{5,6},{6,7},{7,0},{8,9},{9,10},{10,1... | collective-permute-start | bytes 24584 | tf_op jit(solution)/shard_map/while/body/eval_jaxpr/ppermute | solution.py:46
  31.0 34.5 %collective-permute-start.2 = (f32[2048,256]{1,0:T(8,128)S(1)}, f32[2048,256]{1,0:T(8,128)}, u32[]{:S(2)}, u32[]{:S(2)}) collective-permute-start(f32[2048,256]{1,0:T(8,128)S(1)} %broadcast_select_fusion.5), channel_id=1, source_target_pairs={{0,1},{1,2},{2,3},{3,4},{4,5},{5,6},{6,7},{7,0},{8,9},{9,10},{10,1... | collective-permute-start | bytes 6291464 | tf_op jit(solution)/shard_map/while/body/eval_jaxpr/ppermute | solution.py:47
  55.8 9.7 %slice-start = ((s8[8388608]{0:T(1024)(128)(4,1)}), s8[4194304]{0:T(1024)(128)(4,1)S(1)}, s32[]{:S(2)}) async-start(s8[8388608]{0:T(1024)(128)(4,1)} %bitcast.29), calls=%async_computation | async-start | bytes 8388608 | tf_op jit(solution)/shard_map/while
  56.9 8.6 %slice-start.1 = ((s8[8388608]{0:T(1024)(128)(4,1)}), s8[4194304]{0:T(1024)(128)(4,1)S(1)}, s32[]{:S(2)}) async-start(s8[8388608]{0:T(1024)(128)(4,1)} %bitcast.29), calls=%async_computation.1 | async-start | bytes 8388608 | tf_op jit(solution)/shard_map/while
  71.9 14.3 %collective-permute-start = (bf16[2048,256]{1,0:T(8,128)(2,1)}, bf16[2048,256]{1,0:T(8,128)(2,1)S(1)}, u32[]{:S(2)}, u32[]{:S(2)}) collective-permute-start(bf16[2048,256]{1,0:T(8,128)(2,1)} %get-tuple-element.205), channel_id=1, source_target_pairs={{0,1},{1,2},{2,3},{3,4},{4,5},{5,6},{6,7},{7,0},{8,9},{9,10},{10,1... | collective-permute-start | bytes 3145736 | tf_op jit(solution)/shard_map/while/body/eval_jaxpr/ppermute | solution.py:45
  74.4 11.8 %collective-permute-start.1 = (f32[2048]{0:T(1024)S(1)}, f32[2048]{0:T(1024)S(1)}, u32[]{:S(2)}, u32[]{:S(2)}) collective-permute-start(f32[2048]{0:T(1024)S(1)} %get-tuple-element.206), channel_id=1, source_target_pairs={{0,1},{1,2},{2,3},{3,4},{4,5},{5,6},{6,7},{7,0},{8,9},{9,10},{10,1... | collective-permute-start | bytes 24584 | tf_op jit(solution)/shard_map/while/body/eval_jaxpr/ppermute | solution.py:46
  76.1 32.9 %collective-permute-start.2 = (f32[2048,256]{1,0:T(8,128)S(1)}, f32[2048,256]{1,0:T(8,128)}, u32[]{:S(2)}, u32[]{:S(2)}) collective-permute-start(f32[2048,256]{1,0:T(8,128)S(1)} %broadcast_select_fusion.5), channel_id=1, source_target_pairs={{0,1},{1,2},{2,3},{3,4},{4,5},{5,6},{6,7},{7,0},{8,9},{9,10},{10,1... | collective-permute-start | bytes 6291464 | tf_op jit(solution)/shard_map/while/body/eval_jaxpr/ppermute | solution.py:47
  99.3 9.7 %slice-start = ((s8[8388608]{0:T(1024)(128)(4,1)}), s8[4194304]{0:T(1024)(128)(4,1)S(1)}, s32[]{:S(2)}) async-start(s8[8388608]{0:T(1024)(128)(4,1)} %bitcast.29), calls=%async_computation | async-start | bytes 8388608 | tf_op jit(solution)/shard_map/while
  100.4 8.6 %slice-start.1 = ((s8[8388608]{0:T(1024)(128)(4,1)}), s8[4194304]{0:T(1024)(128)(4,1)S(1)}, s32[]{:S(2)}) async-start(s8[8388608]{0:T(1024)(128)(4,1)} %bitcast.29), calls=%async_computation.1 | async-start | bytes 8388608 | tf_op jit(solution)/shard_map/while
  115.4 14.3 %collective-permute-start = (bf16[2048,256]{1,0:T(8,128)(2,1)}, bf16[2048,256]{1,0:T(8,128)(2,1)S(1)}, u32[]{:S(2)}, u32[]{:S(2)}) collective-permute-start(bf16[2048,256]{1,0:T(8,128)(2,1)} %get-tuple-element.205), channel_id=1, source_target_pairs={{0,1},{1,2},{2,3},{3,4},{4,5},{5,6},{6,7},{7,0},{8,9},{9,10},{10,1... | collective-permute-start | bytes 3145736 | tf_op jit(solution)/shard_map/while/body/eval_jaxpr/ppermute | solution.py:45
  117.9 11.8 %collective-permute-start.1 = (f32[2048]{0:T(1024)S(1)}, f32[2048]{0:T(1024)S(1)}, u32[]{:S(2)}, u32[]{:S(2)}) collective-permute-start(f32[2048]{0:T(1024)S(1)} %get-tuple-element.206), channel_id=1, source_target_pairs={{0,1},{1,2},{2,3},{3,4},{4,5},{5,6},{6,7},{7,0},{8,9},{9,10},{10,1... | collective-permute-start | bytes 24584 | tf_op jit(solution)/shard_map/while/body/eval_jaxpr/ppermute | solution.py:46
  119.7 32.9 %collective-permute-start.2 = (f32[2048,256]{1,0:T(8,128)S(1)}, f32[2048,256]{1,0:T(8,128)}, u32[]{:S(2)}, u32[]{:S(2)}) collective-permute-start(f32[2048,256]{1,0:T(8,128)S(1)} %broadcast_select_fusion.5), channel_id=1, source_target_pairs={{0,1},{1,2},{2,3},{3,4},{4,5},{5,6},{6,7},{7,0},{8,9},{9,10},{10,1... | collective-permute-start | bytes 6291464 | tf_op jit(solution)/shard_map/while/body/eval_jaxpr/ppermute | solution.py:47
  142.9 9.7 %slice-start = ((s8[8388608]{0:T(1024)(128)(4,1)}), s8[4194304]{0:T(1024)(128)(4,1)S(1)}, s32[]{:S(2)}) async-start(s8[8388608]{0:T(1024)(128)(4,1)} %bitcast.29), calls=%async_computation | async-start | bytes 8388608 | tf_op jit(solution)/shard_map/while
  144.0 8.6 %slice-start.1 = ((s8[8388608]{0:T(1024)(128)(4,1)}), s8[4194304]{0:T(1024)(128)(4,1)S(1)}, s32[]{:S(2)}) async-start(s8[8388608]{0:T(1024)(128)(4,1)} %bitcast.29), calls=%async_computation.1 | async-start | bytes 8388608 | tf_op jit(solution)/shard_map/while
  159.0 14.3 %collective-permute-start.4 = (bf16[2048,256]{1,0:T(8,128)(2,1)}, bf16[2048,256]{1,0:T(8,128)(2,1)S(1)}, u32[]{:S(2)}, u32[]{:S(2)}) collective-permute-start(bf16[2048,256]{1,0:T(8,128)(2,1)} %get-tuple-element.55), channel_id=1, source_target_pairs={{0,1},{1,2},{2,3},{3,4},{4,5},{5,6},{6,7},{7,0},{8,9},{9,10},{10,1... | collective-permute-start | bytes 3145736 | tf_op jit(solution)/shard_map/ppermute | solution.py:55
  161.5 11.8 %collective-permute-start.3 = (f32[2048]{0:T(1024)S(1)}, f32[2048]{0:T(1024)S(1)}, u32[]{:S(2)}, u32[]{:S(2)}) collective-permute-start(f32[2048]{0:T(1024)S(1)} %get-tuple-element.54), channel_id=1, source_target_pairs={{0,1},{1,2},{2,3},{3,4},{4,5},{5,6},{6,7},{7,0},{8,9},{9,10},{10,1... | collective-permute-start | bytes 24584 | tf_op jit(solution)/shard_map/ppermute | solution.py:56
  161.5 34.3 %collective-permute-start.5 = (f32[2048,256]{1,0:T(8,128)}, f32[2048,256]{1,0:T(8,128)}, u32[]{:S(2)}, u32[]{:S(2)}) collective-permute-start(f32[2048,256]{1,0:T(8,128)} %get-tuple-element.56), channel_id=1, source_target_pairs={{0,1},{1,2},{2,3},{3,4},{4,5},{5,6},{6,7},{7,0},{8,9},{9,10},{10,1... | collective-permute-start | bytes 6291464 | tf_op jit(solution)/shard_map/ppermute | solution.py:57
  200.4 56.8 %collective-permute-start.6 = (f32[2048,256]{1,0:T(8,128)}, f32[2048,256]{1,0:T(8,128)}, u32[]{:S(2)}, u32[]{:S(2)}) collective-permute-start(f32[2048,256]{1,0:T(8,128)} %get-tuple-element.117), channel_id=1, source_target_pairs={{0,4},{1,5},{2,6},{3,7},{4,0},{5,1},{6,2},{7,3},{8,12},{9,13},{10,... | collective-permute-start | bytes 6291464 | tf_op jit(solution)/shard_map/ppermute | solution.py:74
where the time goes:
time: 263 us; the launch traced here: 261 us
  matrix products  115 us (44%)
  blocking collectives  53.4 us (20%)
  waiting for transfers between devices  50.8 us (19%)
  starting transfers between devices  19.9 us (8%)
  other arithmetic  12.2 us (5%)
  local copies, waits for them, and re-layouts  6.23 us (2%)
    dot_general x5, matrix products, pair_weight(): lax.dot_general(host_x, vis_x, (((1,), (1,)), ((), ())), preferred_elemen...  55.9 us
    psum x1, blocking collectives, device_body(): energy = lax.psum(energy_acc, 'row')  53.4 us
    dot_general x4, matrix products, pair_forces(): jnp.dot(weight_bf, vis_x, preferred_element_type=jnp.float32)  27.2 us
    ppermute x3, waiting for transfers between devices, full_step(): vis_q = lax.ppermute(vis_q, 'row', forward)  26.5 us
    dot_general x4, matrix products, pair_forces(): lax.dot_general(weight_bf, host_x, (((0,), (0,)), ((), ())), preferred_el...  23.8 us
    ppermute x1, waiting for transfers between devices, device_body(): vis_acc = lax.ppermute(vis_acc, 'row', forward)  14.1 us
    ppermute x1, waiting for transfers between devices, device_body(): vis_q = lax.ppermute(vis_q, 'row', forward)  10.1 us
    dot_general x1, matrix products, device_body(): jnp.dot(diag_w.astype(jnp.bfloat16), pos_loc, preferred_element_type=jnp....  7.97 us
  transfers between devices with their start and end apart: 13, of which 5 were waited for; matrix products, arithmetic and copies ran while one was open for 30% of the time, Pallas kernels for 0%

commit v1 on v0

v1 whole, which is shorter than its diff:
```python
import functools
import math

import jax
import jax.numpy as jnp
from jax import lax
from jax.experimental import pallas as pl
from jax.experimental.pallas import tpu as pltpu
from jax.sharding import PartitionSpec as P

LANES = 128
QUANT = 256
SUBS = 4
HOST = 512


def kernel(cfg, x_hbm, q_ref, f_ref, e_ref, xs, aux, host_a, host_l, host_s, wts, acc, rsum, ebuf, load_sem, near_sem, relay_sem, sib_sem, aux_sem, e_sem, s_near, s_relay, s_fwd, s_sib, s_aux, s_e):
    groups, rows_dev, ring = cfg
    feat = x_hbm.shape[1]
    log2e = math.log2(math.e)
    dot_scale = 2.0 * log2e / (2.0 * feat)
    sq_scale = -log2e / (2.0 * feat)
    own_groups = rows_dev // (QUANT * SUBS)
    quanta = rows_dev // QUANT
    hosts = rows_dev // HOST
    chunks = rows_dev // LANES
    me = lax.axis_index("row")
    core = me % 2
    sib = me + 1 - 2 * core
    right = (me + 2) % ring
    left = (me + ring - 2) % ring
    right_x = (sib + 2) % ring
    left_x = (sib + ring - 2) % ring
    opp = (me + 4) % ring
    opp_x = (sib + 4) % ring

    def remote(src, dst, send, recv, dev):
        return pltpu.make_async_remote_copy(src_ref=src, dst_ref=dst, send_sem=send, recv_sem=recv, device_id={"row": dev}, device_id_type=pl.DeviceIdType.MESH)

    loads = [pltpu.make_async_copy(x_hbm.at[pl.ds(q * QUANT, QUANT), pl.ds(h * LANES, LANES)], xs.at[q // SUBS, q % SUBS, h], load_sem.at[q, h]) for q in range(quanta) for h in range(2)]
    for load in loads:
        load.start()
    barrier = pltpu.get_barrier_semaphore()
    for peer in (sib, right, left, right_x, left_x, opp, opp_x):
        pl.semaphore_signal(barrier, inc=1, device_id={"row": peer}, device_id_type=pl.DeviceIdType.MESH)
    for load in loads:
        load.wait()
    pl.semaphore_wait(barrier, 7)

    first = own_groups + 1

    def to_right(q):
        return remote(xs.at[q // SUBS, q % SUBS], xs.at[first + q, 0], s_near.at[q, 0], near_sem.at[first + q, 0], right)

    def to_left(q):
        return remote(xs.at[q // SUBS, q % SUBS], xs.at[first + q, 1], s_near.at[q, 1], near_sem.at[first + q, 1], left)

    sib_copies = [
        remote(xs.at[0], xs.at[own_groups], s_sib.at[0], sib_sem.at[0], sib),
        remote(xs.at[1, pl.ds(0, 2)], xs.at[first, pl.ds(2, 2)], s_sib.at[1], sib_sem.at[1], sib),
        remote(xs.at[1, pl.ds(2, 2)], xs.at[groups - 1, pl.ds(0, 2)], s_sib.at[2], sib_sem.at[2], sib),
    ]
    for copy in sib_copies:
        copy.start()
    for q in range(2):
        to_right(q).start()
        to_left(q).start()

    for c in range(chunks):
        g, s, r = c // (2 * SUBS), (c // 2) % SUBS, (c % 2) * LANES
        lo = xs[g, s, 0, pl.ds(r, LANES), :].astype(jnp.float32)
        hi = xs[g, s, 1, pl.ds(r, LANES), :].astype(jnp.float32)
        sq = jnp.sum(lo * lo + hi * hi, axis=1, keepdims=True)
        off = jnp.broadcast_to(sq * sq_scale, (LANES, LANES))
        q_row = q_ref[c : c + 1, :]
        aux[g, s, pl.ds(c % 2, 1), :] = jnp.transpose(off)[0:1, :]
        aux[g, s, pl.ds(2 + c % 2, 1), :] = q_row
        q_col = jnp.transpose(jnp.broadcast_to(q_row, (LANES, LANES)))
        mag = jnp.log(jnp.abs(q_col)) * log2e
        host_a[pl.ds(c * LANES, LANES), :] = off + mag
        host_l[pl.ds(c * LANES, LANES), :] = mag
        host_s[pl.ds(c * LANES, LANES), :] = jnp.where(q_col < 0.0, -1.0, 1.0)
    acc[...] = jnp.zeros_like(acc)
    rsum[...] = jnp.zeros_like(rsum)
    wts[1, ...] = jnp.zeros_like(wts[1, ...])

    far = first + quanta
    half = quanta // 2
    aux_plan = [
        (aux.at[0], aux.at[own_groups], sib),
        (aux.at[1, pl.ds(0, 2)], aux.at[first, pl.ds(2, 2)], sib),
        (aux.at[1, pl.ds(2, 2)], aux.at[groups - 1, pl.ds(0, 2)], sib),
    ]
    for h in range(2):
        aux_plan += [
            (aux.at[h], aux.at[pl.ds(first + half * h, half), 0], right),
            (aux.at[h], aux.at[pl.ds(first + half * h, half), 1], left),
            (aux.at[h], aux.at[pl.ds(first + 1 + half * h, half), 2], right_x),
            (aux.at[h], aux.at[pl.ds(first + 1 + half * h, half), 3], left_x),
            (aux.at[h], aux.at[pl.ds(far, half), h], opp),
            (aux.at[h], aux.at[pl.ds(far + 1, half), 2 + h], opp_x),
        ]
    aux_copies = [remote(src, dst, s_aux.at[n], aux_sem.at[n], dev) for n, (src, dst, dev) in enumerate(aux_plan)]
    for copy in aux_copies:
        copy.start()
    for q in range(2, quanta):
        to_right(q).start()
        to_left(q).start()

    def tile(g, s):
        return jnp.concatenate([xs[g, s, 0], xs[g, s, 1]], axis=1)

    def host_tile(t):
        return jnp.concatenate([tile(t * 2 // SUBS, t * 2 % SUBS), tile((t * 2 + 1) // SUBS, (t * 2 + 1) % SUBS)], axis=0)

    def weights(t, g, slot, diag):
        hx = host_tile(t)
        base = t * HOST
        for s in range(SUBS):
            dots = lax.dot_general(hx, tile(g, s), (((1,), (1,)), ((), ())), preferred_element_type=jnp.float32)
            step = LANES if diag else HOST
            for r in range(0, HOST, step):
                at = pl.ds(base + r, step)
                off, cap, total = host_a[at, :], host_l[at, :], rsum[at, :]
                for c in range(2):
                    power = dots[r : r + step, c * LANES : (c + 1) * LANES] * dot_scale + off + aux[g, s, pl.ds(c, 1), :]
                    w = jnp.exp2(jnp.minimum(power, cap)) * aux[g, s, pl.ds(2 + c, 1), :]
                    if diag and base + r == (g * SUBS + s) * QUANT + c * LANES:
                        same = lax.broadcasted_iota(jnp.int32, w.shape, 0) == lax.broadcasted_iota(jnp.int32, w.shape, 1)
                        w = jnp.where(same, 0.0, w)
                    total = total + w
                    wts[slot, 2 * s + c, pl.ds(r, step), :] = w.astype(jnp.bfloat16)
                rsum[at, :] = total

    def pull(t, g, slot):
        part = None
        for s in range(SUBS):
            w = jnp.concatenate([wts[slot, 2 * s], wts[slot, 2 * s + 1]], axis=1)
            d = jnp.dot(w, tile(g, s), preferred_element_type=jnp.float32)
            part = d if part is None else part + d
        acc[pl.ds(t * HOST, HOST), :] += part

    def group(g, before, diag=False):
        for t in range(hosts):
            if t == 0:
                pull(hosts - 1, before, 1)
            else:
                pull(t - 1, g, (t - 1) % 2)
            weights(t, g, t % 2, diag)

    group(0, 0, True)
    group(1, 0, True)

    def near_in(g, d):
        return remote(xs.at[g, d], xs.at[g, d], s_near.at[0, d], near_sem.at[g, d], me)

    def relay(g):
        return remote(xs.at[g, pl.ds(0, 2)], xs.at[g + 1, pl.ds(2, 2)], s_relay.at[g], relay_sem.at[g + 1], sib)

    def forward_right(g):
        return remote(xs.at[g, 0], xs.at[g + quanta, 0], s_fwd.at[g], near_sem.at[g + quanta, 0], right)

    def forward_left(g):
        return remote(xs.at[g, 1], xs.at[g + half, 1], s_fwd.at[g], near_sem.at[g + half, 1], left)

    last = groups - 1
    for copy in sib_copies:
        copy.wait_recv()
    for copy in aux_copies:
        copy.wait_recv()

    def step(g, carry):
        @pl.when((g >= first) & (g < last))
        def _():
            near_in(g, 0).wait_recv()
            near_in(g, 1).wait_recv()
            relay(g).start()

        @pl.when((g >= first) & (g < first + half))
        def _():
            forward_right(g).start()

        @pl.when((g >= first + half) & (g < first + quanta))
        def _():
            forward_left(g).start()

        @pl.when(g > first)
        def _():
            remote(xs.at[g, pl.ds(2, 2)], xs.at[g, pl.ds(2, 2)], s_relay.at[0], relay_sem.at[g], me).wait_recv()

        group(g, g - 1)
        return carry

    lax.fori_loop(own_groups, groups, step, 0)
    energy = jnp.zeros((8, LANES), jnp.float32)
    for r in range(0, rows_dev, HOST):
        at = pl.ds(r, HOST)
        energy = energy + jnp.sum((rsum[at, :] * host_s[at, :]).reshape(HOST // 8, 8, LANES), axis=0)
    ebuf[me] = energy
    pull(hosts - 1, last, 1)
    e_copies = [remote(ebuf.at[me], ebuf.at[me], s_e.at[d], e_sem.at[d], (me + d) % ring) for d in range(1, ring)]
    for copy in e_copies:
        copy.start()
    for t in range(hosts):
        at = pl.ds(t * HOST, HOST)
        total = jnp.sum(rsum[at, :], axis=1, keepdims=True)
        sign = host_s[at, :] * (1.0 / feat)
        hx = host_tile(t).astype(jnp.float32)
        f_ref[at, :] = (total * hx - acc[at, :]) * jnp.concatenate([sign, sign], axis=1)

    for q in range(quanta):
        to_right(q).wait_send()
        to_left(q).wait_send()
    for copy in sib_copies + aux_copies:
        copy.wait_send()

    def drain(g, carry):
        relay(g).wait_send()
        return carry

    lax.fori_loop(first, last, drain, 0)

    def drain_right(g, carry):
        forward_right(g).wait_send()
        return carry

    lax.fori_loop(first, first + half, drain_right, 0)

    def drain_left(g, carry):
        forward_left(g).wait_send()
        return carry

    lax.fori_loop(first + half, first + quanta, drain_left, 0)
    for copy in e_copies:
        copy.wait()
    whole = ebuf[0]
    for d in range(1, ring):
        whole = whole + ebuf[d]
    e_ref[0] = 0.5 * jnp.sum(whole)


def solution(mesh):
    ring = mesh.shape["row"]

    def device_body(pos, chg):
        rows, feat = pos.shape
        groups = ring * rows // (QUANT * SUBS)
        quanta = rows // QUANT
        assert ring == 8 and feat == 2 * LANES and quanta == 8
        dma = pltpu.SemaphoreType.DMA
        f32 = jnp.float32
        vmem = pltpu.VMEM
        scratch = [
            vmem((groups, SUBS, 2, QUANT, LANES), jnp.bfloat16),
            vmem((groups, SUBS, 4, LANES), f32),
            vmem((rows, LANES), f32),
            vmem((rows, LANES), f32),
            vmem((rows, LANES), f32),
            vmem((2, 2 * SUBS, HOST, LANES), jnp.bfloat16),
            vmem((rows, feat), f32),
            vmem((rows, LANES), f32),
            vmem((ring, 8, LANES), f32),
            dma((quanta, 2)),
            dma((groups, 2)),
            dma((groups,)),
            dma((3,)),
            dma((15,)),
            dma((ring,)),
            dma((quanta, 2)),
            dma((groups,)),
            dma((groups,)),
            dma((3,)),
            dma((15,)),
            dma((ring,)),
        ]
        forces, energy = pl.pallas_call(
            functools.partial(kernel, (groups, rows, ring)),
            out_shape=(jax.ShapeDtypeStruct((rows, feat), f32), jax.ShapeDtypeStruct((1,), f32)),
            in_specs=[pl.BlockSpec(memory_space=pltpu.HBM), pl.BlockSpec(memory_space=pltpu.VMEM)],
            out_specs=(pl.BlockSpec(memory_space=pltpu.VMEM), pl.BlockSpec(memory_space=pltpu.SMEM)),
            scratch_shapes=scratch,
            compiler_params=pltpu.CompilerParams(collective_id=0, has_side_effects=True, vmem_limit_bytes=63 * 2**20 - 2**19),
            name="pair_forces",
        )(pos, chg.reshape(rows // LANES, LANES))
        return forces, energy

    return jax.shard_map(device_body, mesh=mesh, in_specs=(P(("sys", "row"), None), P(("sys", "row"))), out_specs=(P(("sys", "row"), None), P("sys")), check_vma=False)
```

time: 263 us -> 62.3 us (0.24)
  matrix products: 115 us -> 0 us
  Pallas kernels: 0 us -> 56.6 us
  blocking collectives: 53.4 us -> 0 us
  waiting for transfers between devices: 50.8 us -> 0 us
  starting transfers between devices: 19.9 us -> 0 us
  other arithmetic: 12.2 us -> 0 us
  local copies, waits for them, and re-layouts: 6.23 us -> 3.05 us
    dot_general x14 -> x0, matrix products: 115 us -> none  [the longest x5 55.9 us: pair_weight(): lax.dot_general(host_x, vis_x, (((1,), (1,)), ((), ())), preferred_elemen...]
    pallas_call x0 -> x1, Pallas kernels: none -> 56.6 us  [device_body(): pl.pallas_call(functools.partial(kernel, (groups, rows, ring)), out_shape...]
    psum x1 -> x0, blocking collectives: 53.4 us -> none  [device_body(): energy = lax.psum(energy_acc, 'row')]
    ppermute x13 -> x0, waiting for transfers between devices: 50.8 us -> none  [the longest x3 26.5 us: full_step(): vis_q = lax.ppermute(vis_q, 'row', forward)]
    ppermute x13 -> x0, starting transfers between devices: 19.9 us -> none  [the longest x3 7.69 us: full_step(): vis_x = lax.ppermute(vis_x, 'row', forward)]
    div x1 -> x0, other arithmetic: 4.28 us -> none  [device_body(): return ((force_acc + home_acc) / ell_sq, energy.reshape(1))]
    while x6 -> x0, other arithmetic: 3.6 us -> none
    while x18 -> x0, local copies, waits for them, and re-layouts: 3.19 us -> none
  transfers between devices with their start and end apart: 13 -> 0, of which waited for: 5 -> 0; matrix products, arithmetic and copies ran while one was open for 30% -> 0% of each run, Pallas kernels for 0% -> 0%
where the time goes in v1:
time: 62.3 us; the launch traced here: 62 us
  Pallas kernels  56.6 us (91%)
  local copies, waits for them, and re-layouts  3.05 us (5%)
  between operations  2.37 us (4%)
    pallas_call x1, Pallas kernels, device_body(): pl.pallas_call(functools.partial(kernel, (groups, rows, ring)), out_shape...  56.6 us
    unnamed x1, local copies, waits for them, and re-layouts  3.05 us

profile of v1, /device:TPU:113, one launch (start us, length us, event | category | flops | bytes accessed | tf_op | source)
XLA Modules:
  0.0 62.0 jit_solution(954495248408321193)
XLA Ops:
  0.6 56.6 %pair_forces.1 = (f32[2048,256]{1,0:T(8,128)}, f32[1]{0:T(128)}) custom-call(bf16[2048,256]{1,0:T(8,128)(2,1)} %x_hbm.1, f32[16,128]{1,0:T(8,128)} %bitcast.1), custom_call_target="tpu_custom_call" | custom-call | tf_op jit(solution)/shard_map/pair_forces/pallas_call | solution.py:276
  57.2 3.0 %copy.6 = f32[2048,256]{1,0:T(8,128)} copy(f32[2048,256]{1,0:T(8,128)} %get-tuple-element.4) | data formatting | bytes 4194304

commit v2 on v1

v2 whole, which is shorter than its diff:
```python
import functools
import math

import jax
import jax.numpy as jnp
from jax import lax
from jax.experimental import pallas as pl
from jax.experimental.pallas import tpu as pltpu
from jax.sharding import PartitionSpec as P

LANES = 128
QUANT = 256
SUBS = 4
HOST = 512
NEAR = [(0, 2), (2, 2), (4, 2), (6, 2)]
FAR = [(8, 2), (10, 1), (11, 1)]


def kernel(cfg, x_ref, q_ref, f_ref, e_ref, xs, aux, host_a, host_l, host_s, wts, acc, rsum, ebuf, near_sem, far_sem, relay_sem, sib_sem, aux_sem, e_sem, s_near, s_far, s_relay, s_sib, s_aux, s_e):
    groups, rows_dev, ring = cfg
    feat = x_ref.shape[2]
    log2e = math.log2(math.e)
    dot_scale = 2.0 * log2e / (2.0 * feat)
    sq_scale = -log2e / (2.0 * feat)
    own_groups = rows_dev // (QUANT * SUBS)
    quanta = rows_dev // QUANT
    hosts = rows_dev // HOST
    chunks = rows_dev // LANES
    me = lax.axis_index("row")
    core = me % 2
    sib = me + 1 - 2 * core
    right = (me + 2) % ring
    left = (me + ring - 2) % ring
    right_x = (sib + 2) % ring
    left_x = (sib + ring - 2) % ring
    opp = (me + 4) % ring
    opp_x = (sib + 4) % ring

    def remote(src, dst, send, recv, dev):
        return pltpu.make_async_remote_copy(src_ref=src, dst_ref=dst, send_sem=send, recv_sem=recv, device_id={"row": dev}, device_id_type=pl.DeviceIdType.MESH)

    barrier = pltpu.get_barrier_semaphore()
    for peer in (sib, right, left, right_x, left_x, opp, opp_x):
        pl.semaphore_signal(barrier, inc=1, device_id={"row": peer}, device_id_type=pl.DeviceIdType.MESH)

    first = own_groups + 1
    half = quanta // 2
    far = first + quanta
    last = groups - 1

    def both_halves(q, n, group, sub, send, recv, dev):
        return [remote(x_ref.at[pl.ds(q, n), :, pl.ds(h * LANES, LANES)], xs.at[pl.ds(group, n), sub, h], send.at[h], recv.at[h], dev) for h in range(2)]

    def within(q, n, group, sub, send, recv, dev):
        return [remote(x_ref.at[pl.ds(q, n), :, pl.ds(h * LANES, LANES)], xs.at[group, pl.ds(sub, n), h], send.at[h], recv.at[h], dev) for h in range(2)]

    near = {}
    for n, (m, size) in enumerate(NEAR):
        near[first + m] = both_halves(m, size, first + m, 0, s_near.at[n, 0], near_sem.at[n, 0], right) + both_halves((m + half) % quanta, size, first + m, 1, s_near.at[n, 1], near_sem.at[n, 1], left)
    sib_copies = within(0, 4, own_groups, 0, s_sib.at[0], sib_sem.at[0], sib) + within(4, 2, first, 2, s_sib.at[1], sib_sem.at[1], sib) + within(6, 2, last, 0, s_sib.at[2], sib_sem.at[2], sib)
    forward = {}
    for n, (m, size) in enumerate(FAR):
        src, dst = first + m - quanta, first + m
        forward[dst] = [remote(xs.at[pl.ds(src, size), d], xs.at[pl.ds(dst, size), d], s_far.at[n, d], far_sem.at[n, d], (right, left)[d]) for d in range(2)]
    relays = {first + m: remote(xs.at[pl.ds(first + m, size), pl.ds(0, 2)], xs.at[pl.ds(first + m + 1, size), pl.ds(2, 2)], s_relay.at[n], relay_sem.at[n], sib) for n, (m, size) in enumerate(NEAR + FAR)}

    pl.semaphore_wait(barrier, 7)
    starts = list(near)
    for copy in near[starts[0]] + sib_copies + near[starts[1]]:
        copy.start()

    for g in range(own_groups):
        for s in range(SUBS):
            for h in range(2):
                xs[g, s, h] = x_ref[g * SUBS + s, :, h * LANES : (h + 1) * LANES]

    eye = lax.broadcasted_iota(jnp.int32, (LANES, LANES), 0) == lax.broadcasted_iota(jnp.int32, (LANES, LANES), 1)
    for c in range(chunks):
        g, s, r = c // (2 * SUBS), (c // 2) % SUBS, (c % 2) * LANES
        lo = xs[g, s, 0, pl.ds(r, LANES), :].astype(jnp.float32)
        hi = xs[g, s, 1, pl.ds(r, LANES), :].astype(jnp.float32)
        off = jnp.sum(lo * lo + hi * hi, axis=1, keepdims=True) * sq_scale
        q_row = q_ref[c : c + 1, :]
        aux[g, s, pl.ds(c % 2, 1), :] = jnp.sum(jnp.where(eye, off, 0.0), axis=0, keepdims=True)
        aux[g, s, pl.ds(2 + c % 2, 1), :] = q_row
        q_col = jnp.sum(jnp.where(eye, q_row, 0.0), axis=1, keepdims=True)
        mag = jnp.log(jnp.abs(q_col)) * log2e
        wide = (LANES, LANES)
        host_a[pl.ds(c * LANES, LANES), :] = jnp.broadcast_to(off + mag, wide)
        host_l[pl.ds(c * LANES, LANES), :] = jnp.broadcast_to(mag, wide)
        host_s[pl.ds(c * LANES, LANES), :] = jnp.broadcast_to(jnp.where(q_col < 0.0, -1.0, 1.0), wide)
    acc[...] = jnp.zeros_like(acc)
    rsum[...] = jnp.zeros_like(rsum)
    wts[1, ...] = jnp.zeros_like(wts[1, ...])

    aux_plan = [
        (aux.at[0], aux.at[own_groups], sib),
        (aux.at[1, pl.ds(0, 2)], aux.at[first, pl.ds(2, 2)], sib),
        (aux.at[1, pl.ds(2, 2)], aux.at[last, pl.ds(0, 2)], sib),
    ]
    for h in range(2):
        at, turned = first + half * h, first + half * (1 - h)
        aux_plan += [
            (aux.at[h], aux.at[pl.ds(at, half), 0], right),
            (aux.at[h], aux.at[pl.ds(turned, half), 1], left),
            (aux.at[h], aux.at[pl.ds(at + 1, half), 2], right_x),
            (aux.at[h], aux.at[pl.ds(turned + 1, half), 3], left_x),
            (aux.at[h], aux.at[pl.ds(far, half), h], opp),
            (aux.at[h], aux.at[pl.ds(far + 1, half), 2 + h], opp_x),
        ]
    aux_copies = [remote(src, dst, s_aux.at[n], aux_sem.at[n], dev) for n, (src, dst, dev) in enumerate(aux_plan)]
    for copy in aux_copies:
        copy.start()
    for g in starts[2:]:
        for copy in near[g]:
            copy.start()

    def tile(g, s):
        return jnp.concatenate([xs[g, s, 0], xs[g, s, 1]], axis=1)

    def host_tile(t):
        return jnp.concatenate([tile(t * 2 // SUBS, t * 2 % SUBS), tile((t * 2 + 1) // SUBS, (t * 2 + 1) % SUBS)], axis=0)

    def weights(t, subs, slot, diag):
        hx = host_tile(t)
        base = t * HOST
        for n, (g, s) in enumerate(subs):
            dots = lax.dot_general(hx, tile(g, s), (((1,), (1,)), ((), ())), preferred_element_type=jnp.float32)
            step = LANES if diag else HOST
            for r in range(0, HOST, step):
                at = pl.ds(base + r, step)
                off, cap, total = host_a[at, :], host_l[at, :], rsum[at, :]
                for c in range(2):
                    power = dots[r : r + step, c * LANES : (c + 1) * LANES] * dot_scale + off + aux[g, s, pl.ds(c, 1), :]
                    w = jnp.exp2(jnp.minimum(power, cap)) * aux[g, s, pl.ds(2 + c, 1), :]
                    if diag and base + r == (g * SUBS + s) * QUANT + c * LANES:
                        w = jnp.where(eye, 0.0, w)
                    total = total + w
                    wts[slot, 2 * n + c, pl.ds(r, step), :] = w.astype(jnp.bfloat16)
                rsum[at, :] = total

    def pull(t, subs, slot):
        part = None
        for n, (g, s) in enumerate(subs):
            w = jnp.concatenate([wts[slot, 2 * n], wts[slot, 2 * n + 1]], axis=1)
            d = jnp.dot(w, tile(g, s), preferred_element_type=jnp.float32)
            part = d if part is None else part + d
        acc[pl.ds(t * HOST, HOST), :] += part

    def visit(subs, before, diag=False):
        for t in range(hosts):
            if t == 0:
                pull(hosts - 1, before, 1)
            else:
                pull(t - 1, subs, (t - 1) % 2)
            weights(t, subs, t % 2, diag)

    def all_of(g):
        return [(g, s) for s in range(SUBS)]

    visit(all_of(0), all_of(0), True)
    visit(all_of(1), all_of(0), True)
    for copy in sib_copies + aux_copies:
        copy.wait_recv()

    def step(g, carry):
        for at in (*near, *forward):
            if at == last - 1:
                continue

            @pl.when(g == at)
            def _():
                for copy in near.get(at) or forward[at]:
                    copy.wait_recv()
                relays[at].start()
                for dst in forward:
                    src = dst - quanta
                    if at in near and max(a for a in near if a <= src) == at:
                        for copy in forward[dst]:
                            copy.start()

        for at, copy in relays.items():

            @pl.when(g == at + 1)
            def _():
                copy.wait_recv()

        visit(all_of(g), all_of(g - 1))
        return carry

    lax.fori_loop(own_groups, last - 1, step, 0)
    relays[last - 2].wait_recv()
    rest = [(last, 0), (last, 1), (last - 1, 2), (last - 1, 3)]
    visit(rest, all_of(last - 2))
    for copy in forward[last - 1]:
        copy.wait_recv()
    relays[last - 1].start()
    late = [(last - 1, 0), (last - 1, 1)]
    visit(late, rest)
    relays[last - 1].wait_recv()
    end = [(last, 2), (last, 3)]
    visit(end, late)
    energy = jnp.zeros((8, LANES), jnp.float32)
    for r in range(0, rows_dev, HOST):
        at = pl.ds(r, HOST)
        energy = energy + jnp.sum((rsum[at, :] * host_s[at, :]).reshape(HOST // 8, 8, LANES), axis=0)
    ebuf[me] = energy
    pull(hosts - 1, end, 1)
    e_copies = [remote(ebuf.at[me], ebuf.at[me], s_e.at[d], e_sem.at[d], (me + d) % ring) for d in range(1, ring)]
    for copy in e_copies:
        copy.start()
    for t in range(hosts):
        at = pl.ds(t * HOST, HOST)
        total = jnp.sum(rsum[at, :], axis=1, keepdims=True)
        sign = host_s[at, :] * (1.0 / feat)
        hx = host_tile(t).astype(jnp.float32)
        f_ref[at, :] = (total * hx - acc[at, :]) * jnp.concatenate([sign, sign], axis=1)

    for copies in (*near.values(), *forward.values(), sib_copies, aux_copies, relays.values()):
        for copy in copies:
            copy.wait_send()
    for copy in e_copies:
        copy.wait()
    whole = ebuf[0]
    for d in range(1, ring):
        whole = whole + ebuf[d]
    e_ref[0] = 0.5 * jnp.sum(whole)


def solution(mesh):
    ring = mesh.shape["row"]

    def device_body(pos, chg):
        rows, feat = pos.shape
        groups = ring * rows // (QUANT * SUBS)
        quanta = rows // QUANT
        assert ring == 8 and feat == 2 * LANES and quanta == 8
        dma = pltpu.SemaphoreType.DMA
        f32 = jnp.float32
        vmem = pltpu.VMEM
        scratch = [
            vmem((groups, SUBS, 2, QUANT, LANES), jnp.bfloat16),
            vmem((groups, SUBS, 4, LANES), f32),
            vmem((rows, LANES), f32),
            vmem((rows, LANES), f32),
            vmem((rows, LANES), f32),
            vmem((2, 2 * SUBS, HOST, LANES), jnp.bfloat16),
            vmem((rows, feat), f32),
            vmem((rows, LANES), f32),
            vmem((ring, 8, LANES), f32),
        ]
        for _ in range(2):
            scratch += [dma((len(NEAR), 2, 2)), dma((len(FAR), 2)), dma((len(NEAR + FAR),)), dma((3, 2)), dma((15,)), dma((ring,))]
        forces, energy = pl.pallas_call(
            functools.partial(kernel, (groups, rows, ring)),
            out_shape=(jax.ShapeDtypeStruct((rows, feat), f32), jax.ShapeDtypeStruct((1,), f32)),
            in_specs=[pl.BlockSpec(memory_space=pltpu.VMEM), pl.BlockSpec(memory_space=pltpu.VMEM)],
            out_specs=(pl.BlockSpec(memory_space=pltpu.VMEM), pl.BlockSpec(memory_space=pltpu.SMEM)),
            scratch_shapes=scratch,
            compiler_params=pltpu.CompilerParams(collective_id=0, has_side_effects=True, vmem_limit_bytes=40 * 2**20),
            name="pair_forces",
        )(pos.reshape(quanta, QUANT, feat), chg.reshape(rows // LANES, LANES))
        return forces, energy

    return jax.shard_map(device_body, mesh=mesh, in_specs=(P(("sys", "row"), None), P(("sys", "row"))), out_specs=(P(("sys", "row"), None), P("sys")), check_vma=False)
```

time: 62.3 us -> 67.1 us (1.077)
  Pallas kernels: 56.6 us -> 61.2 us
    pallas_call x1, Pallas kernels: 56.6 us -> 61.2 us  [device_body(): pl.pallas_call(functools.partial(kernel, (groups, rows, ring)), out_shape...]
    unnamed x1 -> x5, local copies, waits for them, and re-layouts: 3.05 us -> 3.24 us
where the time goes in v2:
time: 67.1 us; the launch traced here: 66.9 us
  Pallas kernels  61.2 us (91%)
  local copies, waits for them, and re-layouts  3.24 us (5%)
  between operations  2.41 us (4%)
    pallas_call x1, Pallas kernels, device_body(): pl.pallas_call(functools.partial(kernel, (groups, rows, ring)), out_shape...  61.2 us
    unnamed x5, local copies, waits for them, and re-layouts  3.24 us

profile of v2, /device:TPU:113, one launch (start us, length us, event | category | flops | bytes accessed | tf_op | source)
XLA Modules:
  0.0 66.9 jit_solution(10989761370977657177)
XLA Ops:
  0.6 0.0 copy-start
  0.6 1.2 %copy-done = bf16[2048,256]{1,0:T(8,128)(2,1)S(1)} copy-done((bf16[2048,256]{1,0:T(8,128)(2,1)S(1)}, bf16[2048,256]{1,0:T(8,128)(2,1)}, u32[]{:S(2)}) %copy-start) | copy-done | bytes 1048600
  1.9 0.0 copy-start.1
  1.9 0.7 %copy-done.1 = f32[2048]{0:T(1024)S(1)} copy-done((f32[2048]{0:T(1024)S(1)}, f32[2048]{0:T(1024)}, u32[]{:S(2)}) %copy-start.1) | copy-done | bytes 8216
  2.6 61.2 %pair_forces.1 = (f32[2048,256]{1,0:T(8,128)S(1)}, f32[1]{0:T(128)}) custom-call(bf16[8,256,256]{2,1,0:T(8,128)(2,1)S(1)} %bitcast.2, f32[16,128]{1,0:T(8,128)S(1)} %bitcast.3), custom_call_target="tpu_custom_call" | custom-call | tf_op jit(solution)/shard_map/pair_forces/pallas_call | solution.py:254
  63.8 1.3 %copy.6 = f32[2048,256]{1,0:T(8,128)} copy(f32[2048,256]{1,0:T(8,128)S(1)} %get-tuple-element.4) | data formatting | bytes 4194304
Async XLA Ops:
  0.6 1.2 %copy-start = (bf16[2048,256]{1,0:T(8,128)(2,1)S(1)}, bf16[2048,256]{1,0:T(8,128)(2,1)}, u32[]{:S(2)}) copy-start(bf16[2048,256]{1,0:T(8,128)(2,1)} %param.2) | copy-start | bytes 3145732
  1.9 0.7 %copy-start.1 = (f32[2048]{0:T(1024)S(1)}, f32[2048]{0:T(1024)}, u32[]{:S(2)}) copy-start(f32[2048]{0:T(1024)} %param.3) | copy-start | bytes 24580

commit v3 on v2

--- a/solution.py
+++ b/solution.py
@@ -16,9 +16,9 @@
 FAR = [(8, 2), (10, 1), (11, 1)]
 
 
-def kernel(cfg, x_ref, q_ref, f_ref, e_ref, xs, aux, host_a, host_l, host_s, wts, acc, rsum, ebuf, near_sem, far_sem, relay_sem, sib_sem, aux_sem, e_sem, s_near, s_far, s_relay, s_sib, s_aux, s_e):
+def kernel(cfg, x_ref, q_ref, f_ref, e_ref, xs, aux, host_a, host_l, host_s, wts, acc, rsum, ebuf, load_sem, near_sem, far_sem, relay_sem, sib_sem, aux_sem, e_sem, s_near, s_far, s_relay, s_sib, s_aux, s_e):
     groups, rows_dev, ring = cfg
-    feat = x_ref.shape[2]
+    feat = x_ref.shape[1]
     log2e = math.log2(math.e)
     dot_scale = 2.0 * log2e / (2.0 * feat)
     sq_scale = -log2e / (2.0 * feat)
@@ -48,31 +48,33 @@
     far = first + quanta
     last = groups - 1
 
-    def both_halves(q, n, group, sub, send, recv, dev):
-        return [remote(x_ref.at[pl.ds(q, n), :, pl.ds(h * LANES, LANES)], xs.at[pl.ds(group, n), sub, h], send.at[h], recv.at[h], dev) for h in range(2)]
-
-    def within(q, n, group, sub, send, recv, dev):
-        return [remote(x_ref.at[pl.ds(q, n), :, pl.ds(h * LANES, LANES)], xs.at[group, pl.ds(sub, n), h], send.at[h], recv.at[h], dev) for h in range(2)]
+    loads = [pltpu.make_async_copy(x_ref.at[pl.ds(q * QUANT, QUANT), pl.ds(h * LANES, LANES)], xs.at[q // SUBS, q % SUBS, h], load_sem.at[q, h]) for q in (0, 1, 4, 5, 2, 3, 6, 7) for h in range(2)]
+    for load in loads:
+        load.start()
+
+    def own(q, n):
+        return xs.at[q // SUBS, pl.ds(q % SUBS, n)]
 
     near = {}
     for n, (m, size) in enumerate(NEAR):
-        near[first + m] = both_halves(m, size, first + m, 0, s_near.at[n, 0], near_sem.at[n, 0], right) + both_halves((m + half) % quanta, size, first + m, 1, s_near.at[n, 1], near_sem.at[n, 1], left)
-    sib_copies = within(0, 4, own_groups, 0, s_sib.at[0], sib_sem.at[0], sib) + within(4, 2, first, 2, s_sib.at[1], sib_sem.at[1], sib) + within(6, 2, last, 0, s_sib.at[2], sib_sem.at[2], sib)
+        near[first + m] = [remote(own((m + d * half) % quanta, size), xs.at[pl.ds(first + m, size), d], s_near.at[n, d], near_sem.at[n, d], (right, left)[d]) for d in range(2)]
+    sib_copies = [remote(own(q, n), dst, s_sib.at[k], sib_sem.at[k], sib) for k, (q, n, dst) in enumerate([(0, 4, xs.at[own_groups]), (4, 2, xs.at[first, pl.ds(2, 2)]), (6, 2, xs.at[last, pl.ds(0, 2)])])]
     forward = {}
     for n, (m, size) in enumerate(FAR):
         src, dst = first + m - quanta, first + m
         forward[dst] = [remote(xs.at[pl.ds(src, size), d], xs.at[pl.ds(dst, size), d], s_far.at[n, d], far_sem.at[n, d], (right, left)[d]) for d in range(2)]
     relays = {first + m: remote(xs.at[pl.ds(first + m, size), pl.ds(0, 2)], xs.at[pl.ds(first + m + 1, size), pl.ds(2, 2)], s_relay.at[n], relay_sem.at[n], sib) for n, (m, size) in enumerate(NEAR + FAR)}
 
+    starts = list(near)
+    for load in loads[:8]:
+        load.wait()
     pl.semaphore_wait(barrier, 7)
-    starts = list(near)
-    for copy in near[starts[0]] + sib_copies + near[starts[1]]:
-        copy.start()
-
-    for g in range(own_groups):
-        for s in range(SUBS):
-            for h in range(2):
-                xs[g, s, h] = x_ref[g * SUBS + s, :, h * LANES : (h + 1) * LANES]
+    for copy in near[starts[0]]:
+        copy.start()
+    for load in loads[8:]:
+        load.wait()
+    for copy in sib_copies + near[starts[1]]:
+        copy.start()
 
     eye = lax.broadcasted_iota(jnp.int32, (LANES, LANES), 0) == lax.broadcasted_iota(jnp.int32, (LANES, LANES), 1)
     for c in range(chunks):
@@ -248,18 +250,19 @@
             vmem((rows, feat), f32),
             vmem((rows, LANES), f32),
             vmem((ring, 8, LANES), f32),
+            dma((quanta, 2)),
         ]
         for _ in range(2):
-            scratch += [dma((len(NEAR), 2, 2)), dma((len(FAR), 2)), dma((len(NEAR + FAR),)), dma((3, 2)), dma((15,)), dma((ring,))]
+            scratch += [dma((len(NEAR), 2)), dma((len(FAR), 2)), dma((len(NEAR + FAR),)), dma((3,)), dma((15,)), dma((ring,))]
         forces, energy = pl.pallas_call(
             functools.partial(kernel, (groups, rows, ring)),
             out_shape=(jax.ShapeDtypeStruct((rows, feat), f32), jax.ShapeDtypeStruct((1,), f32)),
-            in_specs=[pl.BlockSpec(memory_space=pltpu.VMEM), pl.BlockSpec(memory_space=pltpu.VMEM)],
+            in_specs=[pl.BlockSpec(memory_space=pltpu.HBM), pl.BlockSpec(memory_space=pltpu.VMEM)],
             out_specs=(pl.BlockSpec(memory_space=pltpu.VMEM), pl.BlockSpec(memory_space=pltpu.SMEM)),
             scratch_shapes=scratch,
-            compiler_params=pltpu.CompilerParams(collective_id=0, has_side_effects=True, vmem_limit_bytes=40 * 2**20),
+            compiler_params=pltpu.CompilerParams(collective_id=0, has_side_effects=True, vmem_limit_bytes=63 * 2**20 - 2**19),
             name="pair_forces",
-        )(pos.reshape(quanta, QUANT, feat), chg.reshape(rows // LANES, LANES))
+        )(pos, chg.reshape(rows // LANES, LANES))
         return forces, energy
 
     return jax.shard_map(device_body, mesh=mesh, in_specs=(P(("sys", "row"), None), P(("sys", "row"))), out_specs=(P(("sys", "row"), None), P("sys")), check_vma=False)

time: 67.1 us -> 68.3 us (1.018)
  Pallas kernels: 61.2 us -> 62.6 us
    pallas_call x1, Pallas kernels: 61.2 us -> 62.6 us  [device_body(): pl.pallas_call(functools.partial(kernel, (groups, rows, ring)), out_shape...]
    unnamed x5 -> x1, local copies, waits for them, and re-layouts: 3.24 us -> 3.05 us
where the time goes in v3:
time: 68.3 us; the launch traced here: 68 us
  Pallas kernels  62.6 us (92%)
  local copies, waits for them, and re-layouts  3.05 us (4%)
  between operations  2.37 us (3%)
    pallas_call x1, Pallas kernels, device_body(): pl.pallas_call(functools.partial(kernel, (groups, rows, ring)), out_shape...  62.6 us
    unnamed x1, local copies, waits for them, and re-layouts  3.05 us

profile of v3, /device:TPU:113, one launch (start us, length us, event | category | flops | bytes accessed | tf_op | source)
XLA Modules:
  0.0 68.0 jit_solution(16059155818818392193)
XLA Ops:
  0.6 62.6 %pair_forces.1 = (f32[2048,256]{1,0:T(8,128)}, f32[1]{0:T(128)}) custom-call(bf16[2048,256]{1,0:T(8,128)(2,1)} %x_ref.1, f32[16,128]{1,0:T(8,128)} %bitcast.1), custom_call_target="tpu_custom_call" | custom-call | tf_op jit(solution)/shard_map/pair_forces/pallas_call | solution.py:257
  63.2 3.0 %copy.6 = f32[2048,256]{1,0:T(8,128)} copy(f32[2048,256]{1,0:T(8,128)} %get-tuple-element.4) | data formatting | bytes 4194304

commit v4 on v3

--- a/solution.py
+++ b/solution.py
@@ -12,8 +12,8 @@
 QUANT = 256
 SUBS = 4
 HOST = 512
-NEAR = [(0, 2), (2, 2), (4, 2), (6, 2)]
-FAR = [(8, 2), (10, 1), (11, 1)]
+NEAR = [(m, 1) for m in range(8)]
+FAR = [(m, 1) for m in range(8, 12)]
 
 
 def kernel(cfg, x_ref, q_ref, f_ref, e_ref, xs, aux, host_a, host_l, host_s, wts, acc, rsum, ebuf, load_sem, near_sem, far_sem, relay_sem, sib_sem, aux_sem, e_sem, s_near, s_far, s_relay, s_sib, s_aux, s_e):
@@ -73,7 +73,7 @@
         copy.start()
     for load in loads[8:]:
         load.wait()
-    for copy in sib_copies + near[starts[1]]:
+    for copy in sib_copies:
         copy.start()
 
     eye = lax.broadcasted_iota(jnp.int32, (LANES, LANES), 0) == lax.broadcasted_iota(jnp.int32, (LANES, LANES), 1)
@@ -113,8 +113,9 @@
     aux_copies = [remote(src, dst, s_aux.at[n], aux_sem.at[n], dev) for n, (src, dst, dev) in enumerate(aux_plan)]
     for copy in aux_copies:
         copy.start()
-    for g in starts[2:]:
-        for copy in near[g]:
+
+    def send(at):
+        for copy in near.get(at) or forward[at]:
             copy.start()
 
     def tile(g, s):
@@ -160,7 +161,9 @@
     def all_of(g):
         return [(g, s) for s in range(SUBS)]
 
+    send(first + 1)
     visit(all_of(0), all_of(0), True)
+    send(first + 2)
     visit(all_of(1), all_of(0), True)
     for copy in sib_copies + aux_copies:
         copy.wait_recv()
@@ -175,11 +178,12 @@
                 for copy in near.get(at) or forward[at]:
                     copy.wait_recv()
                 relays[at].start()
-                for dst in forward:
-                    src = dst - quanta
-                    if at in near and max(a for a in near if a <= src) == at:
-                        for copy in forward[dst]:
-                            copy.start()
+
+        for at in range(own_groups, last - first - 1):
+
+            @pl.when(g == at)
+            def _():
+                send(first + 1 + at)
 
         for at, copy in relays.items():
 

time: 68.3 us -> 61 us (0.89)
  Pallas kernels: 62.6 us -> 55.4 us
    pallas_call x1, Pallas kernels: 62.6 us -> 55.4 us  [device_body(): pl.pallas_call(functools.partial(kernel, (groups, rows, ring)), out_shape...]
where the time goes in v4:
time: 61 us; the launch traced here: 60.8 us
  Pallas kernels  55.4 us (91%)
  local copies, waits for them, and re-layouts  3.05 us (5%)
  between operations  2.37 us (4%)
    pallas_call x1, Pallas kernels, device_body(): pl.pallas_call(functools.partial(kernel, (groups, rows, ring)), out_shape...  55.4 us
    unnamed x1, local copies, waits for them, and re-layouts  3.05 us

profile of v4, /device:TPU:113, one launch (start us, length us, event | category | flops | bytes accessed | tf_op | source)
XLA Modules:
  0.0 60.8 jit_solution(14413499014000892614)
XLA Ops:
  0.6 55.4 %pair_forces.1 = (f32[2048,256]{1,0:T(8,128)}, f32[1]{0:T(128)}) custom-call(bf16[2048,256]{1,0:T(8,128)(2,1)} %x_ref.1, f32[16,128]{1,0:T(8,128)} %bitcast.1), custom_call_target="tpu_custom_call" | custom-call | tf_op jit(solution)/shard_map/pair_forces/pallas_call | solution.py:261
  56.0 3.0 %copy.6 = f32[2048,256]{1,0:T(8,128)} copy(f32[2048,256]{1,0:T(8,128)} %get-tuple-element.4) | data formatting | bytes 4194304

commit v5 on v2

v5 whole, which is shorter than its diff:
```python
import functools
import math

import jax
import jax.numpy as jnp
from jax import lax
from jax.experimental import pallas as pl
from jax.experimental.pallas import tpu as pltpu
from jax.sharding import PartitionSpec as P

LANES = 128
QUANT = 256
SUBS = 4
HOST = 512


def kernel(cfg, x_ref, q_ref, f_ref, e_ref, xs, aux, host_a, host_l, host_s, wts, acc, rsum, ebuf, held, head_sem, near_sem, relay_sem, sib_sem, aux_sem, e_sem, s_head, s_near, s_relay, s_sib, s_aux, s_e):
    groups, rows_dev, ring = cfg
    feat = x_ref.shape[2]
    log2e = math.log2(math.e)
    dot_scale = 2.0 * log2e / (2.0 * feat)
    sq_scale = -log2e / (2.0 * feat)
    own_groups = rows_dev // (QUANT * SUBS)
    quanta = rows_dev // QUANT
    hosts = rows_dev // HOST
    chunks = rows_dev // LANES
    me = lax.axis_index("row")
    core = me % 2
    sib = me + 1 - 2 * core
    right = (me + 2) % ring
    left = (me + ring - 2) % ring
    right_x = (sib + 2) % ring
    left_x = (sib + ring - 2) % ring
    opp = (me + 4) % ring
    opp_x = (sib + 4) % ring

    def remote(src, dst, send, recv, dev):
        return pltpu.make_async_remote_copy(src_ref=src, dst_ref=dst, send_sem=send, recv_sem=recv, device_id={"row": dev}, device_id_type=pl.DeviceIdType.MESH)

    barrier = pltpu.get_barrier_semaphore()
    for peer in (sib, right, left, right_x, left_x, opp, opp_x):
        pl.semaphore_signal(barrier, inc=1, device_id={"row": peer}, device_id_type=pl.DeviceIdType.MESH)

    first = own_groups + 1
    half = quanta // 2
    far = first + quanta
    last = groups - 1

    def near(m):
        out = []
        for d in range(2):
            q = (m + d * half) % quanta
            out.append(remote(xs.at[q // SUBS, q % SUBS], xs.at[first + m, d], s_near.at[m, d], near_sem.at[first + m, d], (right, left)[d]))
        return out

    def forward(m):
        return [remote(xs.at[first + m - quanta, d], xs.at[first + m, d], s_near.at[m, d], near_sem.at[first + m, d], (right, left)[d]) for d in range(2)]

    def relay(g):
        return remote(xs.at[g, pl.ds(0, 2)], xs.at[g + 1, pl.ds(2, 2)], s_relay.at[g], relay_sem.at[g + 1], sib)

    def arrive(g):
        for d in range(2):
            remote(xs.at[g, d], xs.at[g, d], s_near.at[0, d], near_sem.at[g, d], me).wait_recv()

    def arrive_relay(g):
        remote(xs.at[g, pl.ds(2, 2)], xs.at[g, pl.ds(2, 2)], s_relay.at[0], relay_sem.at[g], me).wait_recv()

    head = []
    for d in range(2):
        for h in range(2):
            head.append(remote(x_ref.at[d * half, :, pl.ds(h * LANES, LANES)], xs.at[first, d, h], s_head.at[d, h], head_sem.at[d, h], (right, left)[d]))
    sib_copies = []
    for k, (q, n, g, s) in enumerate([(0, 4, own_groups, 0), (4, 2, first, 2), (6, 2, last, 0)]):
        for h in range(2):
            sib_copies.append(remote(x_ref.at[pl.ds(q, n), :, pl.ds(h * LANES, LANES)], xs.at[g, pl.ds(s, n), h], s_sib.at[k, h], sib_sem.at[k, h], sib))
    pl.semaphore_wait(barrier, 7)
    for copy in head + sib_copies:
        copy.start()
    for g in range(own_groups):
        for s in range(SUBS):
            for h in range(2):
                xs[g, s, h] = x_ref[g * SUBS + s, :, h * LANES : (h + 1) * LANES]

    eye = lax.broadcasted_iota(jnp.int32, (LANES, LANES), 0) == lax.broadcasted_iota(jnp.int32, (LANES, LANES), 1)
    for c in range(chunks):
        g, s, r = c // (2 * SUBS), (c // 2) % SUBS, (c % 2) * LANES
        lo = xs[g, s, 0, pl.ds(r, LANES), :].astype(jnp.float32)
        hi = xs[g, s, 1, pl.ds(r, LANES), :].astype(jnp.float32)
        off = jnp.sum(lo * lo + hi * hi, axis=1, keepdims=True) * sq_scale
        q_row = q_ref[c : c + 1, :]
        aux[g, s, pl.ds(c % 2, 1), :] = jnp.sum(jnp.where(eye, off, 0.0), axis=0, keepdims=True)
        aux[g, s, pl.ds(2 + c % 2, 1), :] = q_row
        q_col = jnp.sum(jnp.where(eye, q_row, 0.0), axis=1, keepdims=True)
        mag = jnp.log(jnp.abs(q_col)) * log2e
        wide = (LANES, LANES)
        host_a[pl.ds(c * LANES, LANES), :] = jnp.broadcast_to(off + mag, wide)
        host_l[pl.ds(c * LANES, LANES), :] = jnp.broadcast_to(mag, wide)
        host_s[pl.ds(c * LANES, LANES), :] = jnp.broadcast_to(jnp.where(q_col < 0.0, -1.0, 1.0), wide)

    aux_plan = [
        (aux.at[0], aux.at[own_groups], sib),
        (aux.at[1, pl.ds(0, 2)], aux.at[first, pl.ds(2, 2)], sib),
        (aux.at[1, pl.ds(2, 2)], aux.at[last, pl.ds(0, 2)], sib),
    ]
    for h in range(2):
        at, turned = first + half * h, first + half * (1 - h)
        aux_plan += [
            (aux.at[h], aux.at[pl.ds(at, half), 0], right),
            (aux.at[h], aux.at[pl.ds(turned, half), 1], left),
            (aux.at[h], aux.at[pl.ds(at + 1, half), 2], right_x),
            (aux.at[h], aux.at[pl.ds(turned + 1, half), 3], left_x),
            (aux.at[h], aux.at[pl.ds(far, half), h], opp),
            (aux.at[h], aux.at[pl.ds(far + 1, half), 2 + h], opp_x),
        ]
    aux_copies = [remote(src, dst, s_aux.at[n], aux_sem.at[n], dev) for n, (src, dst, dev) in enumerate(aux_plan)]
    def tile(g, s):
        return jnp.concatenate([xs[g, s, 0], xs[g, s, 1]], axis=1)

    def host_tile(t):
        return jnp.concatenate([tile(t * 2 // SUBS, t * 2 % SUBS), tile((t * 2 + 1) // SUBS, (t * 2 + 1) % SUBS)], axis=0)

    def dots(t, g, s):
        return lax.dot_general(host_tile(t), tile(g, s), (((1,), (1,)), ((), ())), preferred_element_type=jnp.float32)

    def emit(prod, t, n, g, s, slot, diag, fresh):
        base = t * HOST
        step = LANES if diag else HOST
        for r in range(0, HOST, step):
            at = pl.ds(base + r, step)
            off, cap = host_a[at, :], host_l[at, :]
            total = None if fresh else rsum[at, :]
            for c in range(2):
                power = prod(r, step, c) * dot_scale + off + aux[g, s, pl.ds(c, 1), :]
                w = jnp.exp2(jnp.minimum(power, cap)) * aux[g, s, pl.ds(2 + c, 1), :]
                if diag and base + r == (g * SUBS + s) * QUANT + c * LANES:
                    w = jnp.where(eye, 0.0, w)
                total = w if total is None else total + w
                wts[slot, 2 * n + c, pl.ds(r, step), :] = w.astype(jnp.bfloat16)
            rsum[at, :] = total

    def weights(t, subs, slot, diag, fresh):
        for n, (g, s) in enumerate(subs):
            p = dots(t, g, s)
            emit(lambda r, step, c: p[r : r + step, c * LANES : (c + 1) * LANES], t, n, g, s, slot, diag, fresh and n == 0)

    def hold(t, subs):
        for n, (g, s) in enumerate(subs):
            p = dots(t, g, s)
            for c in range(2):
                held[2 * n + c] = p[:, c * LANES : (c + 1) * LANES]

    def finish(t, subs, slot, diag, fresh):
        for n, (g, s) in enumerate(subs):
            emit(lambda r, step, c: held[2 * n + c, pl.ds(r, step), :], t, n, g, s, slot, diag, fresh and n == 0)

    def pull(t, subs, slot, fresh):
        part = None
        for n, (g, s) in enumerate(subs):
            w = jnp.concatenate([wts[slot, 2 * n], wts[slot, 2 * n + 1]], axis=1)
            d = jnp.dot(w, tile(g, s), preferred_element_type=jnp.float32)
            part = d if part is None else part + d
        at = pl.ds(t * HOST, HOST)
        acc[at, :] = part if fresh else acc[at, :] + part

    end_tile = hosts - 1

    def visit(subs, before, diag=False, diag_before=False, fresh=False, fresh_before=False):
        if before:
            finish(end_tile, before, 1, diag_before, fresh_before)
        for t in range(end_tile):
            weights(t, subs, t % 2, diag, fresh)
            if t == 0 and before:
                pull(end_tile, before, 1, fresh_before)
            if t > 0:
                pull(t - 1, subs, (t - 1) % 2, fresh)
        hold(end_tile, subs)
        pull(end_tile - 1, subs, (end_tile - 1) % 2, fresh)

    def all_of(g):
        return [(g, s) for s in range(SUBS)]

    def start(copies):
        for copy in copies:
            copy.start()

    start(near(1))
    visit(all_of(0), None, True, fresh=True)
    start(aux_copies + near(2))
    visit(all_of(1), all_of(0), True, True, fresh_before=True)
    start(near(3))
    for copy in sib_copies + aux_copies:
        copy.wait_recv()
    visit(all_of(2), all_of(1), False, True)

    def step(g, carry):
        @pl.when(g < quanta - 1)
        def _():
            start(near(g + 1))

        @pl.when((g >= quanta - 1) & (g < last - first - 1))
        def _():
            start(forward(g + 1))

        @pl.when(g == first)
        def _():
            for copy in head:
                copy.wait_recv()

        @pl.when(g > first)
        def _():
            arrive(g)
            arrive_relay(g)

        relay(g).start()
        visit(all_of(g), all_of(g - 1))
        return carry

    lax.fori_loop(first, last - 1, step, 0)
    arrive_relay(last - 1)
    rest = [(last, 0), (last, 1), (last - 1, 2), (last - 1, 3)]
    visit(rest, all_of(last - 2))
    arrive(last - 1)
    relay(last - 1).start()
    late = [(last - 1, 0), (last - 1, 1)]
    visit(late, rest)
    arrive_relay(last)
    end = [(last, 2), (last, 3)]
    visit(end, late)
    finish(end_tile, end, 1, False, False)
    energy = jnp.zeros((8, LANES), jnp.float32)
    for r in range(0, rows_dev, HOST):
        at = pl.ds(r, HOST)
        energy = energy + jnp.sum((rsum[at, :] * host_s[at, :]).reshape(HOST // 8, 8, LANES), axis=0)
    ebuf[me] = energy
    pull(end_tile, end, 1, False)
    e_copies = [remote(ebuf.at[me], ebuf.at[me], s_e.at[d], e_sem.at[d], (me + d) % ring) for d in range(1, ring)]
    for copy in e_copies:
        copy.start()
    for t in range(hosts):
        at = pl.ds(t * HOST, HOST)
        total = jnp.sum(rsum[at, :], axis=1, keepdims=True)
        sign = host_s[at, :] * (1.0 / feat)
        hx = host_tile(t).astype(jnp.float32)
        f_ref[at, :] = (total * hx - acc[at, :]) * jnp.concatenate([sign, sign], axis=1)

    for copy in head + sib_copies + aux_copies:
        copy.wait_send()

    def drain(g, carry):
        relay(g).wait_send()
        return carry

    def drain_near(m, carry):
        for copy in near(m):
            copy.wait_send()
        return carry

    def drain_forward(m, carry):
        for copy in forward(m):
            copy.wait_send()
        return carry

    lax.fori_loop(first, last, drain, 0)
    lax.fori_loop(1, quanta, drain_near, 0)
    lax.fori_loop(quanta, last - first, drain_forward, 0)
    for copy in e_copies:
        copy.wait()
    whole = ebuf[0]
    for d in range(1, ring):
        whole = whole + ebuf[d]
    e_ref[0] = 0.5 * jnp.sum(whole)


def solution(mesh):
    ring = mesh.shape["row"]

    def device_body(pos, chg):
        rows, feat = pos.shape
        groups = ring * rows // (QUANT * SUBS)
        quanta = rows // QUANT
        assert ring == 8 and feat == 2 * LANES and quanta == 8
        dma = pltpu.SemaphoreType.DMA
        f32 = jnp.float32
        vmem = pltpu.VMEM
        scratch = [
            vmem((groups, SUBS, 2, QUANT, LANES), jnp.bfloat16),
            vmem((groups, SUBS, 4, LANES), f32),
            vmem((rows, LANES), f32),
            vmem((rows, LANES), f32),
            vmem((rows, LANES), f32),
            vmem((2, 2 * SUBS, HOST, LANES), jnp.bfloat16),
            vmem((rows, feat), f32),
            vmem((rows, LANES), f32),
            vmem((ring, 8, LANES), f32),
            vmem((2 * SUBS, HOST, LANES), f32),
        ]
        for _ in range(2):
            scratch += [dma((2, 2)), dma((groups, 2)), dma((groups,)), dma((3, 2)), dma((15,)), dma((ring,))]
        forces, energy = pl.pallas_call(
            functools.partial(kernel, (groups, rows, ring)),
            out_shape=(jax.ShapeDtypeStruct((rows, feat), f32), jax.ShapeDtypeStruct((1,), f32)),
            in_specs=[pl.BlockSpec(memory_space=pltpu.VMEM), pl.BlockSpec(memory_space=pltpu.VMEM)],
            out_specs=(pl.BlockSpec(memory_space=pltpu.VMEM), pl.BlockSpec(memory_space=pltpu.SMEM)),
            scratch_shapes=scratch,
            compiler_params=pltpu.CompilerParams(collective_id=0, has_side_effects=True, vmem_limit_bytes=40 * 2**20),
            name="pair_forces",
        )(pos.reshape(quanta, QUANT, feat), chg.reshape(rows // LANES, LANES))
        return forces, energy

    return jax.shard_map(device_body, mesh=mesh, in_specs=(P(("sys", "row"), None), P(("sys", "row"))), out_specs=(P(("sys", "row"), None), P("sys")), check_vma=False)
```

time: 67.1 us -> 70.7 us (1.054)
  Pallas kernels: 61.2 us -> 64.9 us
    pallas_call x1, Pallas kernels: 61.2 us -> 64.9 us  [device_body(): pl.pallas_call(functools.partial(kernel, (groups, rows, ring)), out_shape...]
where the time goes in v5:
time: 70.7 us; the launch traced here: 70.6 us
  Pallas kernels  64.9 us (92%)
  local copies, waits for them, and re-layouts  3.24 us (5%)
  between operations  2.41 us (3%)
    pallas_call x1, Pallas kernels, device_body(): pl.pallas_call(functools.partial(kernel, (groups, rows, ring)), out_shape...  64.9 us
    unnamed x5, local copies, waits for them, and re-layouts  3.24 us

profile of v5, /device:TPU:113, one launch (start us, length us, event | category | flops | bytes accessed | tf_op | source)
XLA Modules:
  0.0 70.6 jit_solution(17913381587814182039)
XLA Ops:
  0.6 0.0 copy-start
  0.6 1.2 %copy-done = bf16[2048,256]{1,0:T(8,128)(2,1)S(1)} copy-done((bf16[2048,256]{1,0:T(8,128)(2,1)S(1)}, bf16[2048,256]{1,0:T(8,128)(2,1)}, u32[]{:S(2)}) %copy-start) | copy-done | bytes 1048600
  1.9 0.0 copy-start.1
  1.9 0.7 copy-done.1
  2.6 64.9 %pair_forces.1 = (f32[2048,256]{1,0:T(8,128)S(1)}, f32[1]{0:T(128)}) custom-call(bf16[8,256,256]{2,1,0:T(8,128)(2,1)S(1)} %bitcast.2, f32[16,128]{1,0:T(8,128)S(1)} %bitcast.3), custom_call_target="tpu_custom_call" | custom-call | tf_op jit(solution)/shard_map/pair_forces/pallas_call | solution.py:300
  67.5 1.3 %copy.6 = f32[2048,256]{1,0:T(8,128)} copy(f32[2048,256]{1,0:T(8,128)S(1)} %get-tuple-element.4) | data formatting | bytes 4194304
Async XLA Ops:
  0.6 1.2 %copy-start = (bf16[2048,256]{1,0:T(8,128)(2,1)S(1)}, bf16[2048,256]{1,0:T(8,128)(2,1)}, u32[]{:S(2)}) copy-start(bf16[2048,256]{1,0:T(8,128)(2,1)} %param.2) | copy-start | bytes 3145732
  1.9 0.7 copy-start.1

commit v6 on v5

--- a/solution.py
+++ b/solution.py
@@ -14,7 +14,7 @@
 HOST = 512
 
 
-def kernel(cfg, x_ref, q_ref, f_ref, e_ref, xs, aux, host_a, host_l, host_s, wts, acc, rsum, ebuf, held, head_sem, near_sem, relay_sem, sib_sem, aux_sem, e_sem, s_head, s_near, s_relay, s_sib, s_aux, s_e):
+def kernel(cfg, x_ref, q_ref, f_ref, e_ref, xs, aux, host_a, host_l, host_s, wts, acc, rsum, ebuf, head_sem, near_sem, relay_sem, sib_sem, aux_sem, e_sem, s_head, s_near, s_relay, s_sib, s_aux, s_e):
     groups, rows_dev, ring = cfg
     feat = x_ref.shape[2]
     log2e = math.log2(math.e)
@@ -144,16 +144,6 @@
             p = dots(t, g, s)
             emit(lambda r, step, c: p[r : r + step, c * LANES : (c + 1) * LANES], t, n, g, s, slot, diag, fresh and n == 0)
 
-    def hold(t, subs):
-        for n, (g, s) in enumerate(subs):
-            p = dots(t, g, s)
-            for c in range(2):
-                held[2 * n + c] = p[:, c * LANES : (c + 1) * LANES]
-
-    def finish(t, subs, slot, diag, fresh):
-        for n, (g, s) in enumerate(subs):
-            emit(lambda r, step, c: held[2 * n + c, pl.ds(r, step), :], t, n, g, s, slot, diag, fresh and n == 0)
-
     def pull(t, subs, slot, fresh):
         part = None
         for n, (g, s) in enumerate(subs):
@@ -165,17 +155,13 @@
 
     end_tile = hosts - 1
 
-    def visit(subs, before, diag=False, diag_before=False, fresh=False, fresh_before=False):
-        if before:
-            finish(end_tile, before, 1, diag_before, fresh_before)
-        for t in range(end_tile):
-            weights(t, subs, t % 2, diag, fresh)
-            if t == 0 and before:
-                pull(end_tile, before, 1, fresh_before)
+    def visit(subs, before, diag=False, fresh=False, fresh_before=False):
+        for t in range(hosts):
             if t > 0:
                 pull(t - 1, subs, (t - 1) % 2, fresh)
-        hold(end_tile, subs)
-        pull(end_tile - 1, subs, (end_tile - 1) % 2, fresh)
+            elif before:
+                pull(end_tile, before, 1, fresh_before)
+            weights(t, subs, t % 2, diag, fresh)
 
     def all_of(g):
         return [(g, s) for s in range(SUBS)]
@@ -187,11 +173,9 @@
     start(near(1))
     visit(all_of(0), None, True, fresh=True)
     start(aux_copies + near(2))
-    visit(all_of(1), all_of(0), True, True, fresh_before=True)
-    start(near(3))
+    visit(all_of(1), all_of(0), True, fresh_before=True)
     for copy in sib_copies + aux_copies:
         copy.wait_recv()
-    visit(all_of(2), all_of(1), False, True)
 
     def step(g, carry):
         @pl.when(g < quanta - 1)
@@ -212,11 +196,14 @@
             arrive(g)
             arrive_relay(g)
 
-        relay(g).start()
+        @pl.when(g >= first)
+        def _():
+            relay(g).start()
+
         visit(all_of(g), all_of(g - 1))
         return carry
 
-    lax.fori_loop(first, last - 1, step, 0)
+    lax.fori_loop(own_groups, last - 1, step, 0)
     arrive_relay(last - 1)
     rest = [(last, 0), (last, 1), (last - 1, 2), (last - 1, 3)]
     visit(rest, all_of(last - 2))
@@ -227,7 +214,6 @@
     arrive_relay(last)
     end = [(last, 2), (last, 3)]
     visit(end, late)
-    finish(end_tile, end, 1, False, False)
     energy = jnp.zeros((8, LANES), jnp.float32)
     for r in range(0, rows_dev, HOST):
         at = pl.ds(r, HOST)
@@ -293,7 +279,6 @@
             vmem((rows, feat), f32),
             vmem((rows, LANES), f32),
             vmem((ring, 8, LANES), f32),
-            vmem((2 * SUBS, HOST, LANES), f32),
         ]
         for _ in range(2):
             scratch += [dma((2, 2)), dma((groups, 2)), dma((groups,)), dma((3, 2)), dma((15,)), dma((ring,))]

time: 70.7 us -> 63.2 us (0.89)
  Pallas kernels: 64.9 us -> 57.4 us
    pallas_call x1, Pallas kernels: 64.9 us -> 57.4 us  [device_body(): pl.pallas_call(functools.partial(kernel, (groups, rows, ring)), out_shape...]
where the time goes in v6:
time: 63.2 us; the launch traced here: 63 us
  Pallas kernels  57.4 us (91%)
  local copies, waits for them, and re-layouts  3.24 us (5%)
  between operations  2.41 us (4%)
    pallas_call x1, Pallas kernels, device_body(): pl.pallas_call(functools.partial(kernel, (groups, rows, ring)), out_shape...  57.4 us
    unnamed x5, local copies, waits for them, and re-layouts  3.24 us

profile of v6, /device:TPU:113, one launch (start us, length us, event | category | flops | bytes accessed | tf_op | source)
XLA Modules:
  0.0 63.0 jit_solution(2119891818522458614)
XLA Ops:
  0.6 0.0 copy-start
  0.6 1.2 %copy-done = bf16[2048,256]{1,0:T(8,128)(2,1)S(1)} copy-done((bf16[2048,256]{1,0:T(8,128)(2,1)S(1)}, bf16[2048,256]{1,0:T(8,128)(2,1)}, u32[]{:S(2)}) %copy-start) | copy-done | bytes 1048600
  1.9 0.0 copy-start.1
  1.9 0.7 %copy-done.1 = f32[2048]{0:T(1024)S(1)} copy-done((f32[2048]{0:T(1024)S(1)}, f32[2048]{0:T(1024)}, u32[]{:S(2)}) %copy-start.1) | copy-done | bytes 8216
  2.6 57.4 %pair_forces.1 = (f32[2048,256]{1,0:T(8,128)S(1)}, f32[1]{0:T(128)}) custom-call(bf16[8,256,256]{2,1,0:T(8,128)(2,1)S(1)} %bitcast.2, f32[16,128]{1,0:T(8,128)S(1)} %bitcast.3), custom_call_target="tpu_custom_call" | custom-call | tf_op jit(solution)/shard_map/pair_forces/pallas_call | solution.py:285
  59.9 1.3 %copy.6 = f32[2048,256]{1,0:T(8,128)} copy(f32[2048,256]{1,0:T(8,128)S(1)} %get-tuple-element.4) | data formatting | bytes 4194304
Async XLA Ops:
  0.6 1.2 %copy-start = (bf16[2048,256]{1,0:T(8,128)(2,1)S(1)}, bf16[2048,256]{1,0:T(8,128)(2,1)}, u32[]{:S(2)}) copy-start(bf16[2048,256]{1,0:T(8,128)(2,1)} %param.2) | copy-start | bytes 3145732
  1.9 0.7 %copy-start.1 = (f32[2048]{0:T(1024)S(1)}, f32[2048]{0:T(1024)}, u32[]{:S(2)}) copy-start(f32[2048]{0:T(1024)} %param.3) | copy-start | bytes 24580

commit v7 on v6

--- a/solution.py
+++ b/solution.py
@@ -46,47 +46,46 @@
     far = first + quanta
     last = groups - 1
 
-    def near(m):
-        out = []
-        for d in range(2):
-            q = (m + d * half) % quanta
-            out.append(remote(xs.at[q // SUBS, q % SUBS], xs.at[first + m, d], s_near.at[m, d], near_sem.at[first + m, d], (right, left)[d]))
-        return out
-
-    def forward(m):
-        return [remote(xs.at[first + m - quanta, d], xs.at[first + m, d], s_near.at[m, d], near_sem.at[first + m, d], (right, left)[d]) for d in range(2)]
+    def hop(m, turn):
+        d = (core + turn) % 2
+        on = m // quanta
+        src = (1 - on) * ((m + d * half) % quanta) + on * ((first + m - quanta) * SUBS + d)
+        dst = (first + m) * SUBS + d
+        return remote(xs.at[src], xs.at[dst], s_near.at[m, d], near_sem.at[first + m, d], (me + 2 + d * (ring - 4)) % ring)
+
+    def hop_first(turn):
+        d = (core + turn) % 2
+        return [remote(x_ref.at[d * half, :, pl.ds(h * LANES, LANES)], xs.at[first * SUBS + d, h], s_head.at[d, h], head_sem.at[d, h], (me + 2 + d * (ring - 4)) % ring) for h in range(2)]
 
     def relay(g):
-        return remote(xs.at[g, pl.ds(0, 2)], xs.at[g + 1, pl.ds(2, 2)], s_relay.at[g], relay_sem.at[g + 1], sib)
+        return remote(xs.at[pl.ds(g * SUBS, 2)], xs.at[pl.ds((g + 1) * SUBS + 2, 2)], s_relay.at[g], relay_sem.at[g + 1], sib)
 
     def arrive(g):
         for d in range(2):
-            remote(xs.at[g, d], xs.at[g, d], s_near.at[0, d], near_sem.at[g, d], me).wait_recv()
+            remote(xs.at[g * SUBS + d], xs.at[g * SUBS + d], s_near.at[0, d], near_sem.at[g, d], me).wait_recv()
 
     def arrive_relay(g):
-        remote(xs.at[g, pl.ds(2, 2)], xs.at[g, pl.ds(2, 2)], s_relay.at[0], relay_sem.at[g], me).wait_recv()
-
-    head = []
-    for d in range(2):
+        at = pl.ds(g * SUBS + 2, 2)
+        remote(xs.at[at], xs.at[at], s_relay.at[0], relay_sem.at[g], me).wait_recv()
+
+    sib_copies = []
+    for k, (q, n, at) in enumerate([(0, 4, own_groups * SUBS), (4, 2, first * SUBS + 2), (6, 2, last * SUBS)]):
         for h in range(2):
-            head.append(remote(x_ref.at[d * half, :, pl.ds(h * LANES, LANES)], xs.at[first, d, h], s_head.at[d, h], head_sem.at[d, h], (right, left)[d]))
-    sib_copies = []
-    for k, (q, n, g, s) in enumerate([(0, 4, own_groups, 0), (4, 2, first, 2), (6, 2, last, 0)]):
-        for h in range(2):
-            sib_copies.append(remote(x_ref.at[pl.ds(q, n), :, pl.ds(h * LANES, LANES)], xs.at[g, pl.ds(s, n), h], s_sib.at[k, h], sib_sem.at[k, h], sib))
+            sib_copies.append(remote(x_ref.at[pl.ds(q, n), :, pl.ds(h * LANES, LANES)], xs.at[pl.ds(at, n), h], s_sib.at[k, h], sib_sem.at[k, h], sib))
+    head = hop_first(0) + hop_first(1)
     pl.semaphore_wait(barrier, 7)
-    for copy in head + sib_copies:
+    for copy in head[:2] + sib_copies:
         copy.start()
     for g in range(own_groups):
         for s in range(SUBS):
             for h in range(2):
-                xs[g, s, h] = x_ref[g * SUBS + s, :, h * LANES : (h + 1) * LANES]
+                xs[g * SUBS + s, h] = x_ref[g * SUBS + s, :, h * LANES : (h + 1) * LANES]
 
     eye = lax.broadcasted_iota(jnp.int32, (LANES, LANES), 0) == lax.broadcasted_iota(jnp.int32, (LANES, LANES), 1)
     for c in range(chunks):
         g, s, r = c // (2 * SUBS), (c // 2) % SUBS, (c % 2) * LANES
-        lo = xs[g, s, 0, pl.ds(r, LANES), :].astype(jnp.float32)
-        hi = xs[g, s, 1, pl.ds(r, LANES), :].astype(jnp.float32)
+        lo = xs[g * SUBS + s, 0, pl.ds(r, LANES), :].astype(jnp.float32)
+        hi = xs[g * SUBS + s, 1, pl.ds(r, LANES), :].astype(jnp.float32)
         off = jnp.sum(lo * lo + hi * hi, axis=1, keepdims=True) * sq_scale
         q_row = q_ref[c : c + 1, :]
         aux[g, s, pl.ds(c % 2, 1), :] = jnp.sum(jnp.where(eye, off, 0.0), axis=0, keepdims=True)
@@ -115,7 +114,7 @@
         ]
     aux_copies = [remote(src, dst, s_aux.at[n], aux_sem.at[n], dev) for n, (src, dst, dev) in enumerate(aux_plan)]
     def tile(g, s):
-        return jnp.concatenate([xs[g, s, 0], xs[g, s, 1]], axis=1)
+        return jnp.concatenate([xs[g * SUBS + s, 0], xs[g * SUBS + s, 1]], axis=1)
 
     def host_tile(t):
         return jnp.concatenate([tile(t * 2 // SUBS, t * 2 % SUBS), tile((t * 2 + 1) // SUBS, (t * 2 + 1) % SUBS)], axis=0)
@@ -155,13 +154,15 @@
 
     end_tile = hosts - 1
 
-    def visit(subs, before, diag=False, fresh=False, fresh_before=False):
+    def visit(subs, before, diag=False, fresh=False, fresh_before=False, sends=None):
         for t in range(hosts):
             if t > 0:
                 pull(t - 1, subs, (t - 1) % 2, fresh)
             elif before:
                 pull(end_tile, before, 1, fresh_before)
             weights(t, subs, t % 2, diag, fresh)
+            if sends is not None and t == hosts // 2 - 1:
+                hop(sends, 1).start()
 
     def all_of(g):
         return [(g, s) for s in range(SUBS)]
@@ -170,21 +171,18 @@
         for copy in copies:
             copy.start()
 
-    start(near(1))
-    visit(all_of(0), None, True, fresh=True)
-    start(aux_copies + near(2))
-    visit(all_of(1), all_of(0), True, fresh_before=True)
+    start(head[2:] + [hop(1, 0)])
+    visit(all_of(0), None, True, fresh=True, sends=1)
+    start(aux_copies + [hop(2, 0)])
+    visit(all_of(1), all_of(0), True, fresh_before=True, sends=2)
     for copy in sib_copies + aux_copies:
         copy.wait_recv()
 
     def step(g, carry):
-        @pl.when(g < quanta - 1)
-        def _():
-            start(near(g + 1))
-
-        @pl.when((g >= quanta - 1) & (g < last - first - 1))
-        def _():
-            start(forward(g + 1))
+        m = g + 1
+        for turn in range(2):
+            hop(m - 2, turn).wait_send()
+        hop(m, 0).start()
 
         @pl.when(g == first)
         def _():
@@ -200,10 +198,20 @@
         def _():
             relay(g).start()
 
+        visit(all_of(g), all_of(g - 1), sends=m)
+        return carry
+
+    sends_end = last - first - 1
+    lax.fori_loop(own_groups, sends_end, step, 0)
+
+    def step_late(g, carry):
+        arrive(g)
+        arrive_relay(g)
+        relay(g).start()
         visit(all_of(g), all_of(g - 1))
         return carry
 
-    lax.fori_loop(own_groups, last - 1, step, 0)
+    lax.fori_loop(sends_end, last - 1, step_late, 0)
     arrive_relay(last - 1)
     rest = [(last, 0), (last, 1), (last - 1, 2), (last - 1, 3)]
     visit(rest, all_of(last - 2))
@@ -237,19 +245,10 @@
         relay(g).wait_send()
         return carry
 
-    def drain_near(m, carry):
-        for copy in near(m):
-            copy.wait_send()
-        return carry
-
-    def drain_forward(m, carry):
-        for copy in forward(m):
-            copy.wait_send()
-        return carry
-
     lax.fori_loop(first, last, drain, 0)
-    lax.fori_loop(1, quanta, drain_near, 0)
-    lax.fori_loop(quanta, last - first, drain_forward, 0)
+    for m in range(sends_end - 1, sends_end + 1):
+        for turn in range(2):
+            hop(m, turn).wait_send()
     for copy in e_copies:
         copy.wait()
     whole = ebuf[0]
@@ -270,7 +269,7 @@
         f32 = jnp.float32
         vmem = pltpu.VMEM
         scratch = [
-            vmem((groups, SUBS, 2, QUANT, LANES), jnp.bfloat16),
+            vmem((groups * SUBS, 2, QUANT, LANES), jnp.bfloat16),
             vmem((groups, SUBS, 4, LANES), f32),
             vmem((rows, LANES), f32),
             vmem((rows, LANES), f32),

time: 63.2 us -> 64.8 us (1.025)
  Pallas kernels: 57.4 us -> 59 us
    pallas_call x1, Pallas kernels: 57.4 us -> 59 us  [device_body(): pl.pallas_call(functools.partial(kernel, (groups, rows, ring)), out_shape...]
where the time goes in v7:
time: 64.8 us; the launch traced here: 64.6 us
  Pallas kernels  59 us (91%)
  local copies, waits for them, and re-layouts  3.24 us (5%)
  between operations  2.41 us (4%)
    pallas_call x1, Pallas kernels, device_body(): pl.pallas_call(functools.partial(kernel, (groups, rows, ring)), out_shape...  59 us
    unnamed x5, local copies, waits for them, and re-layouts  3.24 us

profile of v7, /device:TPU:113, one launch (start us, length us, event | category | flops | bytes accessed | tf_op | source)
XLA Modules:
  0.0 64.6 jit_solution(16186171716492949403)
XLA Ops:
  0.6 0.0 copy-start
  0.6 1.2 %copy-done = bf16[2048,256]{1,0:T(8,128)(2,1)S(1)} copy-done((bf16[2048,256]{1,0:T(8,128)(2,1)S(1)}, bf16[2048,256]{1,0:T(8,128)(2,1)}, u32[]{:S(2)}) %copy-start) | copy-done | bytes 1048600
  1.9 0.0 copy-start.1
  1.9 0.7 %copy-done.1 = f32[2048]{0:T(1024)S(1)} copy-done((f32[2048]{0:T(1024)S(1)}, f32[2048]{0:T(1024)}, u32[]{:S(2)}) %copy-start.1) | copy-done | bytes 8216
  2.6 59.0 %pair_forces.1 = (f32[2048,256]{1,0:T(8,128)S(1)}, f32[1]{0:T(128)}) custom-call(bf16[8,256,256]{2,1,0:T(8,128)(2,1)S(1)} %bitcast.2, f32[16,128]{1,0:T(8,128)S(1)} %bitcast.3), custom_call_target="tpu_custom_call" | custom-call | tf_op jit(solution)/shard_map/pair_forces/pallas_call | solution.py:284
  61.5 1.3 %copy.6 = f32[2048,256]{1,0:T(8,128)} copy(f32[2048,256]{1,0:T(8,128)S(1)} %get-tuple-element.4) | data formatting | bytes 4194304
Async XLA Ops:
  0.6 1.2 %copy-start = (bf16[2048,256]{1,0:T(8,128)(2,1)S(1)}, bf16[2048,256]{1,0:T(8,128)(2,1)}, u32[]{:S(2)}) copy-start(bf16[2048,256]{1,0:T(8,128)(2,1)} %param.2) | copy-start | bytes 3145732
  1.9 0.7 %copy-start.1 = (f32[2048]{0:T(1024)S(1)}, f32[2048]{0:T(1024)}, u32[]{:S(2)}) copy-start(f32[2048]{0:T(1024)} %param.3) | copy-start | bytes 24580

commit v8 on v7

--- a/solution.py
+++ b/solution.py
@@ -74,7 +74,7 @@
             sib_copies.append(remote(x_ref.at[pl.ds(q, n), :, pl.ds(h * LANES, LANES)], xs.at[pl.ds(at, n), h], s_sib.at[k, h], sib_sem.at[k, h], sib))
     head = hop_first(0) + hop_first(1)
     pl.semaphore_wait(barrier, 7)
-    for copy in head[:2] + sib_copies:
+    for copy in head + sib_copies:
         copy.start()
     for g in range(own_groups):
         for s in range(SUBS):
@@ -154,15 +154,13 @@
 
     end_tile = hosts - 1
 
-    def visit(subs, before, diag=False, fresh=False, fresh_before=False, sends=None):
+    def visit(subs, before, diag=False, fresh=False, fresh_before=False):
         for t in range(hosts):
             if t > 0:
                 pull(t - 1, subs, (t - 1) % 2, fresh)
             elif before:
                 pull(end_tile, before, 1, fresh_before)
             weights(t, subs, t % 2, diag, fresh)
-            if sends is not None and t == hosts // 2 - 1:
-                hop(sends, 1).start()
 
     def all_of(g):
         return [(g, s) for s in range(SUBS)]
@@ -171,43 +169,38 @@
         for copy in copies:
             copy.start()
 
-    start(head[2:] + [hop(1, 0)])
-    visit(all_of(0), None, True, fresh=True, sends=1)
-    start(aux_copies + [hop(2, 0)])
-    visit(all_of(1), all_of(0), True, fresh_before=True, sends=2)
+    def hops(m):
+        return [hop(m, 0), hop(m, 1)]
+
+    start(aux_copies + hops(1))
+    visit(all_of(0), None, True, fresh=True)
+    start(hops(2))
+    visit(all_of(1), all_of(0), True, fresh_before=True)
+    start(hops(3))
     for copy in sib_copies + aux_copies:
         copy.wait_recv()
+    visit(all_of(2), all_of(1))
+    start(hops(4))
+    for copy in head:
+        copy.wait_recv()
+    relay(first).start()
+    visit(all_of(first), all_of(first - 1))
 
     def step(g, carry):
-        m = g + 1
-        for turn in range(2):
-            hop(m - 2, turn).wait_send()
-        hop(m, 0).start()
-
-        @pl.when(g == first)
-        def _():
-            for copy in head:
-                copy.wait_recv()
-
-        @pl.when(g > first)
-        def _():
-            arrive(g)
-            arrive_relay(g)
-
-        @pl.when(g >= first)
-        def _():
-            relay(g).start()
-
-        visit(all_of(g), all_of(g - 1), sends=m)
+        start(hops(g + 1))
+        arrive(g)
+        relay(g).start()
+        arrive_relay(g)
+        visit(all_of(g), all_of(g - 1))
         return carry
 
     sends_end = last - first - 1
-    lax.fori_loop(own_groups, sends_end, step, 0)
+    lax.fori_loop(first + 1, sends_end, step, 0)
 
     def step_late(g, carry):
         arrive(g)
+        relay(g).start()
         arrive_relay(g)
-        relay(g).start()
         visit(all_of(g), all_of(g - 1))
         return carry
 
@@ -246,9 +239,12 @@
         return carry
 
     lax.fori_loop(first, last, drain, 0)
-    for m in range(sends_end - 1, sends_end + 1):
-        for turn in range(2):
-            hop(m, turn).wait_send()
+    def drain_hops(m, carry):
+        for copy in hops(m):
+            copy.wait_send()
+        return carry
+
+    lax.fori_loop(1, sends_end + 1, drain_hops, 0)
     for copy in e_copies:
         copy.wait()
     whole = ebuf[0]

time: 64.8 us -> 60.2 us (0.929)
  Pallas kernels: 59 us -> 54.3 us
    pallas_call x1, Pallas kernels: 59 us -> 54.3 us  [device_body(): pl.pallas_call(functools.partial(kernel, (groups, rows, ring)), out_shape...]
where the time goes in v8:
time: 60.2 us; the launch traced here: 60 us
  Pallas kernels  54.3 us (90%)
  local copies, waits for them, and re-layouts  3.24 us (5%)
  between operations  2.41 us (4%)
    pallas_call x1, Pallas kernels, device_body(): pl.pallas_call(functools.partial(kernel, (groups, rows, ring)), out_shape...  54.3 us
    unnamed x5, local copies, waits for them, and re-layouts  3.24 us

profile of v8, /device:TPU:113, one launch (start us, length us, event | category | flops | bytes accessed | tf_op | source)
XLA Modules:
  0.0 60.0 jit_solution(5927609867430509432)
XLA Ops:
  0.6 0.0 copy-start
  0.6 1.2 %copy-done = bf16[2048,256]{1,0:T(8,128)(2,1)S(1)} copy-done((bf16[2048,256]{1,0:T(8,128)(2,1)S(1)}, bf16[2048,256]{1,0:T(8,128)(2,1)}, u32[]{:S(2)}) %copy-start) | copy-done | bytes 1048600
  1.9 0.0 copy-start.1
  1.9 0.7 %copy-done.1 = f32[2048]{0:T(1024)S(1)} copy-done((f32[2048]{0:T(1024)S(1)}, f32[2048]{0:T(1024)}, u32[]{:S(2)}) %copy-start.1) | copy-done | bytes 8216
  2.6 54.3 %pair_forces.1 = (f32[2048,256]{1,0:T(8,128)S(1)}, f32[1]{0:T(128)}) custom-call(bf16[8,256,256]{2,1,0:T(8,128)(2,1)S(1)} %bitcast.2, f32[16,128]{1,0:T(8,128)S(1)} %bitcast.3), custom_call_target="tpu_custom_call" | custom-call | tf_op jit(solution)/shard_map/pair_forces/pallas_call | solution.py:280
  56.9 1.3 %copy.6 = f32[2048,256]{1,0:T(8,128)} copy(f32[2048,256]{1,0:T(8,128)S(1)} %get-tuple-element.4) | data formatting | bytes 4194304
Async XLA Ops:
  0.6 1.2 %copy-start = (bf16[2048,256]{1,0:T(8,128)(2,1)S(1)}, bf16[2048,256]{1,0:T(8,128)(2,1)}, u32[]{:S(2)}) copy-start(bf16[2048,256]{1,0:T(8,128)(2,1)} %param.2) | copy-start | bytes 3145732
  1.9 0.7 %copy-start.1 = (f32[2048]{0:T(1024)S(1)}, f32[2048]{0:T(1024)}, u32[]{:S(2)}) copy-start(f32[2048]{0:T(1024)} %param.3) | copy-start | bytes 24580

commit v9 on v8

--- a/solution.py
+++ b/solution.py
@@ -172,29 +172,29 @@
     def hops(m):
         return [hop(m, 0), hop(m, 1)]
 
-    start(aux_copies + hops(1))
+    start(aux_copies + hops(1) + hops(2))
     visit(all_of(0), None, True, fresh=True)
-    start(hops(2))
+    start(hops(3))
     visit(all_of(1), all_of(0), True, fresh_before=True)
-    start(hops(3))
+    start(hops(4) + hops(5))
     for copy in sib_copies + aux_copies:
         copy.wait_recv()
     visit(all_of(2), all_of(1))
-    start(hops(4))
+    start(hops(6))
     for copy in head:
         copy.wait_recv()
     relay(first).start()
     visit(all_of(first), all_of(first - 1))
 
     def step(g, carry):
-        start(hops(g + 1))
+        start(hops(g + 3))
         arrive(g)
         relay(g).start()
         arrive_relay(g)
         visit(all_of(g), all_of(g - 1))
         return carry
 
-    sends_end = last - first - 1
+    sends_end = last - first - 3
     lax.fori_loop(first + 1, sends_end, step, 0)
 
     def step_late(g, carry):
@@ -244,7 +244,7 @@
             copy.wait_send()
         return carry
 
-    lax.fori_loop(1, sends_end + 1, drain_hops, 0)
+    lax.fori_loop(1, sends_end + 3, drain_hops, 0)
     for copy in e_copies:
         copy.wait()
     whole = ebuf[0]

time: 60.2 us -> 60 us (level)
  no operation moved by 1% of the time
where the time goes in v9:
time: 60 us; the launch traced here: 59.9 us
  Pallas kernels  54.2 us (90%)
  local copies, waits for them, and re-layouts  3.24 us (5%)
  between operations  2.41 us (4%)
    pallas_call x1, Pallas kernels, device_body(): pl.pallas_call(functools.partial(kernel, (groups, rows, ring)), out_shape...  54.2 us
    unnamed x5, local copies, waits for them, and re-layouts  3.24 us

profile of v9, /device:TPU:113, one launch (start us, length us, event | category | flops | bytes accessed | tf_op | source)
XLA Modules:
  0.0 59.9 jit_solution(3509421399662350926)
XLA Ops:
  0.6 0.0 copy-start
  0.6 1.2 %copy-done = bf16[2048,256]{1,0:T(8,128)(2,1)S(1)} copy-done((bf16[2048,256]{1,0:T(8,128)(2,1)S(1)}, bf16[2048,256]{1,0:T(8,128)(2,1)}, u32[]{:S(2)}) %copy-start) | copy-done | bytes 1048600
  1.9 0.0 copy-start.1
  1.9 0.7 %copy-done.1 = f32[2048]{0:T(1024)S(1)} copy-done((f32[2048]{0:T(1024)S(1)}, f32[2048]{0:T(1024)}, u32[]{:S(2)}) %copy-start.1) | copy-done | bytes 8216
  2.6 54.2 %pair_forces.1 = (f32[2048,256]{1,0:T(8,128)S(1)}, f32[1]{0:T(128)}) custom-call(bf16[8,256,256]{2,1,0:T(8,128)(2,1)S(1)} %bitcast.2, f32[16,128]{1,0:T(8,128)S(1)} %bitcast.3), custom_call_target="tpu_custom_call" | custom-call | tf_op jit(solution)/shard_map/pair_forces/pallas_call | solution.py:280
  56.8 1.3 %copy.6 = f32[2048,256]{1,0:T(8,128)} copy(f32[2048,256]{1,0:T(8,128)S(1)} %get-tuple-element.4) | data formatting | bytes 4194304
Async XLA Ops:
  0.6 1.2 %copy-start = (bf16[2048,256]{1,0:T(8,128)(2,1)S(1)}, bf16[2048,256]{1,0:T(8,128)(2,1)}, u32[]{:S(2)}) copy-start(bf16[2048,256]{1,0:T(8,128)(2,1)} %param.2) | copy-start | bytes 3145732
  1.9 0.7 %copy-start.1 = (f32[2048]{0:T(1024)S(1)}, f32[2048]{0:T(1024)}, u32[]{:S(2)}) copy-start(f32[2048]{0:T(1024)} %param.3) | copy-start | bytes 24580

commit v10 on v9

--- a/solution.py
+++ b/solution.py
@@ -73,9 +73,6 @@
         for h in range(2):
             sib_copies.append(remote(x_ref.at[pl.ds(q, n), :, pl.ds(h * LANES, LANES)], xs.at[pl.ds(at, n), h], s_sib.at[k, h], sib_sem.at[k, h], sib))
     head = hop_first(0) + hop_first(1)
-    pl.semaphore_wait(barrier, 7)
-    for copy in head + sib_copies:
-        copy.start()
     for g in range(own_groups):
         for s in range(SUBS):
             for h in range(2):
@@ -96,6 +93,10 @@
         host_a[pl.ds(c * LANES, LANES), :] = jnp.broadcast_to(off + mag, wide)
         host_l[pl.ds(c * LANES, LANES), :] = jnp.broadcast_to(mag, wide)
         host_s[pl.ds(c * LANES, LANES), :] = jnp.broadcast_to(jnp.where(q_col < 0.0, -1.0, 1.0), wide)
+
+    pl.semaphore_wait(barrier, 7)
+    for copy in head + sib_copies:
+        copy.start()
 
     aux_plan = [
         (aux.at[0], aux.at[own_groups], sib),
@@ -220,16 +221,20 @@
         at = pl.ds(r, HOST)
         energy = energy + jnp.sum((rsum[at, :] * host_s[at, :]).reshape(HOST // 8, 8, LANES), axis=0)
     ebuf[me] = energy
-    pull(end_tile, end, 1, False)
-    e_copies = [remote(ebuf.at[me], ebuf.at[me], s_e.at[d], e_sem.at[d], (me + d) % ring) for d in range(1, ring)]
-    for copy in e_copies:
-        copy.start()
-    for t in range(hosts):
+    def result(t):
         at = pl.ds(t * HOST, HOST)
         total = jnp.sum(rsum[at, :], axis=1, keepdims=True)
         sign = host_s[at, :] * (1.0 / feat)
         hx = host_tile(t).astype(jnp.float32)
         f_ref[at, :] = (total * hx - acc[at, :]) * jnp.concatenate([sign, sign], axis=1)
+
+    result(0)
+    e_copies = [remote(ebuf.at[me], ebuf.at[me], s_e.at[d], e_sem.at[d], (me + d) % ring) for d in range(1, ring)]
+    for copy in e_copies:
+        copy.start()
+    pull(end_tile, end, 1, False)
+    for t in range(1, hosts):
+        result(t)
 
     for copy in head + sib_copies + aux_copies:
         copy.wait_send()

time: 60 us -> 59.8 us (level)
  no operation moved by 1% of the time
where the time goes in v10:
time: 59.8 us; the launch traced here: 59.7 us
  Pallas kernels  54 us (90%)
  local copies, waits for them, and re-layouts  3.24 us (5%)
  between operations  2.41 us (4%)
    pallas_call x1, Pallas kernels, device_body(): pl.pallas_call(functools.partial(kernel, (groups, rows, ring)), out_shape...  54 us
    unnamed x5, local copies, waits for them, and re-layouts  3.24 us

profile of v10, /device:TPU:113, one launch (start us, length us, event | category | flops | bytes accessed | tf_op | source)
XLA Modules:
  0.0 59.7 jit_solution(11065735010454449467)
XLA Ops:
  0.6 0.0 copy-start
  0.6 1.2 %copy-done = bf16[2048,256]{1,0:T(8,128)(2,1)S(1)} copy-done((bf16[2048,256]{1,0:T(8,128)(2,1)S(1)}, bf16[2048,256]{1,0:T(8,128)(2,1)}, u32[]{:S(2)}) %copy-start) | copy-done | bytes 1048600
  1.9 0.0 copy-start.1
  1.9 0.7 %copy-done.1 = f32[2048]{0:T(1024)S(1)} copy-done((f32[2048]{0:T(1024)S(1)}, f32[2048]{0:T(1024)}, u32[]{:S(2)}) %copy-start.1) | copy-done | bytes 8216
  2.6 54.0 %pair_forces.1 = (f32[2048,256]{1,0:T(8,128)S(1)}, f32[1]{0:T(128)}) custom-call(bf16[8,256,256]{2,1,0:T(8,128)(2,1)S(1)} %bitcast.2, f32[16,128]{1,0:T(8,128)S(1)} %bitcast.3), custom_call_target="tpu_custom_call" | custom-call | tf_op jit(solution)/shard_map/pair_forces/pallas_call | solution.py:285
  56.6 1.3 %copy.6 = f32[2048,256]{1,0:T(8,128)} copy(f32[2048,256]{1,0:T(8,128)S(1)} %get-tuple-element.4) | data formatting | bytes 4194304
Async XLA Ops:
  0.6 1.2 %copy-start = (bf16[2048,256]{1,0:T(8,128)(2,1)S(1)}, bf16[2048,256]{1,0:T(8,128)(2,1)}, u32[]{:S(2)}) copy-start(bf16[2048,256]{1,0:T(8,128)(2,1)} %param.2) | copy-start | bytes 3145732
  1.9 0.7 %copy-start.1 = (f32[2048]{0:T(1024)S(1)}, f32[2048]{0:T(1024)}, u32[]{:S(2)}) copy-start(f32[2048]{0:T(1024)} %param.3) | copy-start | bytes 24580

commit v11 on v10

--- a/solution.py
+++ b/solution.py
@@ -14,7 +14,7 @@
 HOST = 512
 
 
-def kernel(cfg, x_ref, q_ref, f_ref, e_ref, xs, aux, host_a, host_l, host_s, wts, acc, rsum, ebuf, head_sem, near_sem, relay_sem, sib_sem, aux_sem, e_sem, s_head, s_near, s_relay, s_sib, s_aux, s_e):
+def kernel(cfg, x_ref, q_ref, f_ref, e_ref, xs, aux, host_a, host_l, host_s, wts, acc, rsum, ebuf, head_sem, near_sem, relay_sem, sib_sem, aux_sem, e_sem, s_head, s_near, s_relay, s_sib, s_aux, s_e, s_cross):
     groups, rows_dev, ring = cfg
     feat = x_ref.shape[2]
     log2e = math.log2(math.e)
@@ -53,6 +53,11 @@
         dst = (first + m) * SUBS + d
         return remote(xs.at[src], xs.at[dst], s_near.at[m, d], near_sem.at[first + m, d], (me + 2 + d * (ring - 4)) % ring)
 
+    def cross(m, d):
+        src = (first + m - quanta + 1) * SUBS + 2 + d
+        dst = (first + m) * SUBS + d
+        return remote(xs.at[src], xs.at[dst], s_cross.at[m, d], near_sem.at[first + m, d], (sib + 2 + d * (ring - 4)) % ring)
+
     def hop_first(turn):
         d = (core + turn) % 2
         return [remote(x_ref.at[d * half, :, pl.ds(h * LANES, LANES)], xs.at[first * SUBS + d, h], s_head.at[d, h], head_sem.at[d, h], (me + 2 + d * (ring - 4)) % ring) for h in range(2)]
@@ -188,7 +193,16 @@
     visit(all_of(first), all_of(first - 1))
 
     def step(g, carry):
-        start(hops(g + 3))
+        m = g + 3
+
+        @pl.when(m < quanta)
+        def _():
+            start(hops(m))
+
+        @pl.when((m >= quanta) & (core == 1))
+        def _():
+            start(hops(m) + [cross(m, 0), cross(m, 1)])
+
         arrive(g)
         relay(g).start()
         arrive_relay(g)
@@ -249,7 +263,14 @@
             copy.wait_send()
         return carry
 
-    lax.fori_loop(1, sends_end + 3, drain_hops, 0)
+    lax.fori_loop(1, quanta, drain_hops, 0)
+
+    @pl.when(core == 1)
+    def _():
+        for m in range(quanta, sends_end + 3):
+            for copy in hops(m) + [cross(m, 0), cross(m, 1)]:
+                copy.wait_send()
+
     for copy in e_copies:
         copy.wait()
     whole = ebuf[0]
@@ -282,6 +303,7 @@
         ]
         for _ in range(2):
             scratch += [dma((2, 2)), dma((groups, 2)), dma((groups,)), dma((3, 2)), dma((15,)), dma((ring,))]
+        scratch.append(dma((groups, 2)))
         forces, energy = pl.pallas_call(
             functools.partial(kernel, (groups, rows, ring)),
             out_shape=(jax.ShapeDtypeStruct((rows, feat), f32), jax.ShapeDtypeStruct((1,), f32)),

time: 59.8 us -> 60 us (level)
  no operation moved by 1% of the time
where the time goes in v11:
time: 60 us; the launch traced here: 59.8 us
  Pallas kernels  54.2 us (90%)
  local copies, waits for them, and re-layouts  3.24 us (5%)
  between operations  2.41 us (4%)
    pallas_call x1, Pallas kernels, device_body(): pl.pallas_call(functools.partial(kernel, (groups, rows, ring)), out_shape...  54.2 us
    unnamed x5, local copies, waits for them, and re-layouts  3.24 us

profile of v11, /device:TPU:113, one launch (start us, length us, event | category | flops | bytes accessed | tf_op | source)
XLA Modules:
  0.0 59.8 jit_solution(12614732337499262731)
XLA Ops:
  0.6 0.0 copy-start
  0.6 1.2 %copy-done = bf16[2048,256]{1,0:T(8,128)(2,1)S(1)} copy-done((bf16[2048,256]{1,0:T(8,128)(2,1)S(1)}, bf16[2048,256]{1,0:T(8,128)(2,1)}, u32[]{:S(2)}) %copy-start) | copy-done | bytes 1048600
  1.9 0.0 copy-start.1
  1.9 0.7 %copy-done.1 = f32[2048]{0:T(1024)S(1)} copy-done((f32[2048]{0:T(1024)S(1)}, f32[2048]{0:T(1024)}, u32[]{:S(2)}) %copy-start.1) | copy-done | bytes 8216
  2.6 54.2 %pair_forces.1 = (f32[2048,256]{1,0:T(8,128)S(1)}, f32[1]{0:T(128)}) custom-call(bf16[8,256,256]{2,1,0:T(8,128)(2,1)S(1)} %bitcast.2, f32[16,128]{1,0:T(8,128)S(1)} %bitcast.3), custom_call_target="tpu_custom_call" | custom-call | tf_op jit(solution)/shard_map/pair_forces/pallas_call | solution.py:307
  56.7 1.3 %copy.6 = f32[2048,256]{1,0:T(8,128)} copy(f32[2048,256]{1,0:T(8,128)S(1)} %get-tuple-element.4) | data formatting | bytes 4194304
Async XLA Ops:
  0.6 1.2 %copy-start = (bf16[2048,256]{1,0:T(8,128)(2,1)S(1)}, bf16[2048,256]{1,0:T(8,128)(2,1)}, u32[]{:S(2)}) copy-start(bf16[2048,256]{1,0:T(8,128)(2,1)} %param.2) | copy-start | bytes 3145732
  1.9 0.7 %copy-start.1 = (f32[2048]{0:T(1024)S(1)}, f32[2048]{0:T(1024)}, u32[]{:S(2)}) copy-start(f32[2048]{0:T(1024)} %param.3) | copy-start | bytes 24580
